TPU v7x, 128 devices: a whole 4x4x4 slice. The times are simulated.
128 devices in a mesh: slab: 4 (over x_hi, core), img: 32 (over z, y, x_lo).
Axes of the slice: x: 4 (x_hi: 2, x_lo: 2; x = x_hi * 2 + x_lo), y: 4, z: 4, core: 2. Of those that a mesh axis runs over, the one named last changes fastest.
Arguments:
- feats: bfloat16 [32, 32, 128, 512], P('img', 'slab'), may hold values from -6 to 6
- labels: int32 [32], P('img'), may hold values from 0 to 999
- conv_w: bfloat16 [9, 512, 4], replicated, may hold values from -0.09375 to 0.09375
- embed_w: bfloat16 [16, 1024], replicated, may hold values from -1.5 to 1.5
- mod_table: bfloat16 [1000, 2048], replicated, may hold values from -3 to 3
- qkv_w: bfloat16 [1024, 3072], replicated, may hold values from -0.1875 to 0.1875
- out_w: bfloat16 [1024, 1024], replicated, may hold values from -0.1875 to 0.1875
- proj_w: bfloat16 [1024, 768], replicated, may hold values from -0.1875 to 0.1875
- dino: bfloat16 [32, 1024, 768], P('img', 'slab'), may hold values from -6 to 6
Outputs:
- grad_feats: bfloat16 [32, 32, 128, 512], P('img', 'slab')
- grad_proj: float32 [1024, 768], replicated
- grad_conv: float32 [9, 512, 4], replicated
- loss: float32 [], replicated
All inputs are finite; a program needn't handle non-finite values.
Results may differ from a plain program's by a relative error of at most 0.024.
Values may be sent and summed in bfloat16 or wider, within the bound.
No kernel may reach another device: no remote copies, remote signals or barrier semaphores. Data moves between devices by JAX's collectives and lax.ppermute only.
A program may use at most 128 MiB of HBM per device.

v0:
```python
import jax
import jax.numpy as jnp
from jax import lax
from jax.sharding import PartitionSpec as P

HEAD_DIM = 64


latent_scale = 0.18215
norm_eps = 1e-06
cosine_eps = 1e-06


def extended(cells, sides, width):
    for axis, dim in sides:
        count = lax.axis_size(axis)
        ends = count - 1
        head = lax.slice_in_dim(cells, 0, width, axis=dim)
        tail = lax.slice_in_dim(cells, cells.shape[dim] - width, cells.shape[dim], axis=dim)
        cells = jnp.concatenate(
            [
                lax.ppermute(tail, axis, [(i, (i + 1) % count) for i in range(ends)]),
                cells,
                lax.ppermute(head, axis, [((i + 1) % count, i) for i in range(ends)]),
            ],
            axis=dim,
        )
    return cells


def sent_together(arrays, axis, dim, along):
    widths = [a.shape[along] for a in arrays]
    both = jnp.concatenate(arrays, axis=along)
    out = lax.all_gather(both, axis, axis=dim, tiled=True)
    return tuple(jnp.split(out, [sum(widths[:k]) for k in range(1, len(widths))], axis=along))


def together(arrays, axis):
    ends = [0]
    for a in arrays:
        ends.append(ends[-1] + a.size)
    subtotal = lax.psum(jnp.concatenate([a.ravel() for a in arrays]), axis)
    return tuple((subtotal[b:e].reshape(a.shape) for a, b, e in zip(arrays, ends, ends[1:])))


def conv_out(padded, conv_w):
    rows = padded.shape[0] - 2
    cols = padded.shape[1] - 2
    total = jnp.zeros((rows * cols, conv_w.shape[2]), jnp.float32)
    for tap in range(9):
        view = padded[tap // 3 : tap // 3 + rows, tap % 3 : tap % 3 + cols]
        total = total + jnp.dot(
            view.reshape(rows * cols, -1), conv_w[tap], preferred_element_type=jnp.float32
        )
    return total.reshape(rows, cols, -1) * latent_scale


def contract_first(left, right):
    return lax.dot_general(
        left, right, (((0,), (0,)), ((), ())), preferred_element_type=jnp.float32
    )


def contract_last(left, right):
    return lax.dot_general(
        left, right, (((1,), (1,)), ((), ())), preferred_element_type=jnp.float32
    )


def conv_back(padded, grad_pad, conv_w):
    rows = grad_pad.shape[0] - 2
    cols = grad_pad.shape[1] - 2
    center = grad_pad[1:-1, 1:-1].reshape(rows * cols, -1)
    grad_in = jnp.zeros((rows * cols, conv_w.shape[1]), jnp.float32)
    parts = []
    for tap in range(9):
        row_off = tap // 3
        col_off = tap % 3
        g_view = grad_pad[
            2 - row_off : 2 - row_off + rows, 2 - col_off : 2 - col_off + cols
        ].reshape(rows * cols, -1)
        grad_in = grad_in + contract_last(g_view, conv_w[tap])
        f_view = padded[row_off : row_off + rows, col_off : col_off + cols].reshape(rows * cols, -1)
        parts.append(contract_first(f_view, center))
    return (grad_in.reshape(rows, cols, -1), jnp.stack(parts, 0))


def patchify(latent):
    rows, cols, chans = latent.shape
    blocks = latent.reshape(rows // 2, 2, cols // 2, 2, chans).transpose(0, 2, 1, 3, 4)
    return blocks.reshape(rows // 2 * (cols // 2), 4 * chans)


def unpatchify(tokens, rows, cols):
    chans = tokens.shape[1] // 4
    blocks = tokens.reshape(rows // 2, cols // 2, 2, 2, chans).transpose(0, 2, 1, 3, 4)
    return blocks.reshape(rows, cols, chans)


def cosine_grad(projected, target):
    norm_p = jnp.sqrt(jnp.sum(projected * projected, -1, keepdims=True) + cosine_eps)
    norm_t = jnp.sqrt(jnp.sum(target * target, -1, keepdims=True) + cosine_eps)
    cosine = jnp.sum(projected * target, -1, keepdims=True) / (norm_p * norm_t)
    grad = cosine * projected / (norm_p * norm_p) - target / (norm_p * norm_t)
    return (cosine[:, 0], grad)


def local(feats, labels, conv_w, embed_w, mod_table, qkv_w, out_w, proj_w, dino):
    image = feats[0]
    rows, cols, chans = image.shape
    width = qkv_w.shape[0]
    heads = width // HEAD_DIM
    scale = HEAD_DIM ** (-0.5)
    rimmed = extended(image, (("slab", 0),), 1)
    padded = jnp.pad(rimmed, ((0, 0), (1, 1), (0, 0)))
    tokens = patchify(conv_out(padded, conv_w))
    count = tokens.shape[0]
    embed_f = embed_w.astype(jnp.float32)
    start = jnp.dot(tokens, embed_f, precision=lax.Precision.HIGHEST)
    row = lax.dynamic_index_in_dim(mod_table, labels[0], 0, keepdims=False).astype(jnp.float32)
    mean = jnp.mean(start, -1, keepdims=True)
    cent = start - mean
    inv = lax.rsqrt(jnp.mean(cent * cent, -1, keepdims=True) + norm_eps)
    normed = cent * inv
    modded = (normed * (1.0 + row[width:]) + row[:width]).astype(jnp.bfloat16)
    qkv = jnp.dot(modded, qkv_w, preferred_element_type=jnp.float32).astype(jnp.bfloat16)
    query = qkv[:, :width]
    key = qkv[:, width : 2 * width]
    value = qkv[:, 2 * width :]
    key_all, value_all = sent_together((key, value), "slab", 0, 1)
    q3 = query.reshape(count, heads, HEAD_DIM)
    k3 = key_all.reshape(-1, heads, HEAD_DIM)
    v3 = value_all.reshape(-1, heads, HEAD_DIM)
    scores = jnp.einsum("qhd,khd->hqk", q3, k3, preferred_element_type=jnp.float32) * scale
    top = jnp.max(scores, -1, keepdims=True)
    expo = jnp.exp(scores - top)
    total = jnp.sum(expo, -1)
    attended = (
        jnp.einsum(
            "hqk,khd->qhd", expo.astype(jnp.bfloat16), v3, preferred_element_type=jnp.float32
        )
        / total.T[:, :, None]
    )
    attended = attended.reshape(count, width).astype(jnp.bfloat16)
    lse = top[..., 0] + jnp.log(total)
    resid = start + jnp.dot(attended, out_w, preferred_element_type=jnp.float32)
    resid_b = resid.astype(jnp.bfloat16)
    projected = jnp.dot(resid_b, proj_w, preferred_element_type=jnp.float32)
    cosine, grad_p = cosine_grad(projected, dino[0].astype(jnp.float32))
    grad_pb = grad_p.astype(jnp.bfloat16)
    proj_part = contract_first(resid_b, grad_pb)
    grad_resid = contract_last(grad_pb, proj_w)
    grad_att = contract_last(grad_resid.astype(jnp.bfloat16), out_w).astype(jnp.bfloat16)
    g3 = grad_att.reshape(count, heads, HEAD_DIM)
    delta = jnp.sum(
        g3.astype(jnp.float32) * attended.reshape(count, heads, HEAD_DIM).astype(jnp.float32), -1
    ).T
    probs = jnp.exp(scores - lse[..., None])
    dprobs = jnp.einsum("qhd,khd->hqk", g3, v3, preferred_element_type=jnp.float32)
    dscores = (probs * (dprobs - delta[..., None])).astype(jnp.bfloat16)
    grad_query = scale * jnp.einsum(
        "hqk,khd->qhd", dscores, k3, preferred_element_type=jnp.float32
    ).reshape(count, width)
    query_all, grad_all = sent_together((query, grad_att), "slab", 0, 1)
    lse_all, delta_all = tuple(
        (
            part.astype(jnp.float32)
            for part in sent_together(
                (lse.astype(jnp.bfloat16), delta.astype(jnp.bfloat16)), "slab", 1, 0
            )
        )
    )
    qa3 = query_all.reshape(-1, heads, HEAD_DIM)
    ga3 = grad_all.reshape(-1, heads, HEAD_DIM)
    own_keys = key.reshape(count, heads, HEAD_DIM)
    own_values = value.reshape(count, heads, HEAD_DIM)
    far_scores = (
        jnp.einsum("qhd,khd->hqk", qa3, own_keys, preferred_element_type=jnp.float32) * scale
    )
    far_probs = jnp.exp(far_scores - lse_all[..., None])
    far_dprobs = jnp.einsum("qhd,khd->hqk", ga3, own_values, preferred_element_type=jnp.float32)
    far_dscores = (far_probs * (far_dprobs - delta_all[..., None])).astype(jnp.bfloat16)
    grad_key = scale * jnp.einsum(
        "hqk,qhd->khd", far_dscores, qa3, preferred_element_type=jnp.float32
    ).reshape(count, width)
    grad_value = jnp.einsum(
        "hqk,qhd->khd", far_probs.astype(jnp.bfloat16), ga3, preferred_element_type=jnp.float32
    ).reshape(count, width)
    grad_qkv = jnp.concatenate([grad_query, grad_key, grad_value], 1).astype(jnp.bfloat16)
    grad_mod = contract_last(grad_qkv, qkv_w)
    grad_norm = grad_mod * (1.0 + row[width:])
    grad_start = grad_resid + inv * (
        grad_norm
        - jnp.mean(grad_norm, -1, keepdims=True)
        - normed * jnp.mean(grad_norm * normed, -1, keepdims=True)
    )
    grad_tokens = jnp.dot(grad_start, embed_f.T, precision=lax.Precision.HIGHEST)
    grad_latent = (unpatchify(grad_tokens, rows, cols) * latent_scale).astype(jnp.bfloat16)
    grad_rim = extended(grad_latent, (("slab", 0),), 1)
    grad_pad = jnp.pad(grad_rim, ((0, 0), (1, 1), (0, 0)))
    grad_image, conv_part = conv_back(padded, grad_pad, conv_w)
    loss_part = jnp.sum(1.0 - cosine)
    grad_proj, grad_conv, loss_sum = together((proj_part, conv_part, loss_part), ("slab", "img"))
    groups = lax.axis_size("slab") * lax.axis_size("img")
    return (
        grad_image.astype(jnp.bfloat16)[None],
        grad_proj,
        grad_conv,
        loss_sum / (groups * count),
    )


def solution(mesh):
    in_specs = (
        P("img", "slab", None, None),
        P("img"),
        P(),
        P(),
        P(),
        P(),
        P(),
        P(),
        P("img", "slab", None),
    )
    out_specs = (P("img", "slab", None, None), P(), P(), P())
    return jax.shard_map(local, mesh=mesh, in_specs=in_specs, out_specs=out_specs, check_vma=False)
```

profile of v0, /device:TPU:1, one launch (start us, length us, event | category | flops | bytes accessed | tf_op | source)
XLA Modules:
  0.0 384.0 jit_solution(8328961745691364285)
XLA Ops:
  7.2 1.1 slice_bitcast_fusion.1
  8.4 6.0 %collective-permute-start = (bf16[1,128,512]{2,1,0:T(8,128)(2,1)S(1)}, bf16[1,128,512]{2,1,0:T(8,128)(2,1)S(1)}, u32[]{:S(2)}, u32[]{:S(2)}) collective-permute-start(bf16[1,128,512]{2,1,0:T(8,128)(2,1)S(1)} %get-tuple-element.37), channel_id=1, source_target_pairs={{0,32},{32,64},{64,96},{1,33},{33,65},{65,97},{2,34},{34,66},{66,9... | collective-permute-start | bytes 393224 | tf_op jit(solution)/shard_map/ppermute | solution.py:22
  14.4 1.9 collective-permute-start.1
  17.0 1.6 fusion.118
  20.0 2.2 collective-permute-done.1
  22.8 1.7 fusion.24
  29.7 1.2 copy.54
  31.7 1.4 fusion.174
  33.4 4.7 %convolution_convert_fusion = bf16[256,3072]{1,0:T(8,128)(2,1)S(1)} fusion(bf16[1024,3072]{1,0:T(8,128)(2,1)} %param.14, f32[256,1024]{1,0:T(8,128)S(1)} %get-tuple-element.47, f32[1024]{0:T(1024)S(1)} %bitcast.275, f32[1024]{0:T(1024)S(1)} %bitcast.274, f32[256]{0:T(256)S(1)} %add_rsqrt_fusion, f32[256]{0:T(256)S(1)} %broadcast_multiply_fusion.2), kind=kOutput, calls=%fused_computation.16 | convolution fusion | flops 1612709888 | bytes 8923136 | tf_op jit(solution)/shard_map/dot_general | solution.py:126
  38.2 1.1 copy-done.20
  39.3 1.1 concatenate.45
  40.7 2.6 fusion.171
  43.2 2.0 copy.56
  45.3 34.9 %all-gather.3.cloned.1.call-done = bf16[1024,2048]{1,0:T(8,128)(2,1)} async-done(((bf16[256,2048]{1,0:T(8,128)(2,1)}), bf16[1024,2048]{1,0:T(8,128)(2,1)}) %all-gather.3.cloned.1.call-update) | async-done | bytes 4194320 | tf_op jit(solution)/shard_map/all_gather | solution.py:34
  80.2 4.7 %fusion.170 = (bf16[1024,1024]{1,0:T(8,128)(2,1)}, bf16[1024,1024]{1,0:T(8,128)(2,1)}) fusion(bf16[1024,2048]{1,0:T(8,128)(2,1)} %all-gather.3.cloned.1.call-done), kind=kLoop, calls=%fused_computation.212 | loop fusion | bytes 8388608 | tf_op jit(solution)/shard_map/split | solution.py:35
  84.9 3.9 %copy.57 = bf16[1024,1024]{0,1:T(8,128)(2,1)} copy(bf16[1024,1024]{1,0:T(8,128)(2,1)} %get-tuple-element.24) | data formatting | bytes 4194304 | tf_op jit(solution)/shard_map/split | solution.py:35
  88.9 3.9 %copy.55 = bf16[1024,1024]{0,1:T(8,128)(2,1)} copy(bf16[1024,1024]{1,0:T(8,128)(2,1)} %get-tuple-element.25) | data formatting | bytes 4194304 | tf_op jit(solution)/shard_map/split | solution.py:35
  92.8 4.2 %multiply_reduce_fusion = (f32[16,256]{1,0:T(8,128)S(1)}, f32[16,256,1024]{2,1,0:T(8,128)S(1)}) fusion(bf16[256,16,64]{0,2,1:T(8,128)(2,1)} %bitcast.262, bf16[1024,16,64]{0,2,1:T(8,128)(2,1)} %bitcast.239), kind=kOutput, calls=%fused_computation.7 | convolution fusion | flops 545255424 | bytes 19415040 | tf_op jit(solution)/shard_map/qhd,khd->hqk/dot_general | solution.py:134
  97.1 3.6 fusion
  100.7 2.6 copy-done.3
  103.4 3.8 divide_convert_fusion
  118.6 2.3 fusion.177
  120.9 4.6 %reshape.257 = f32[786432]{0:T(1024)} reshape(f32[1024,768]{1,0:T(8,128)} %fusion.177) | data formatting | bytes 6291456 | tf_op jit(solution)/shard_map/reshape | solution.py:42
  125.5 1.4 multiply_reduce_fusion.2
  127.6 7.6 %all_gather.11 = bf16[32,1024]{1,0:T(8,128)(2,1)S(1)} all-gather(bf16[32,256]{1,0:T(8,128)(2,1)S(1)} %pad_maximum_fusion.4), channel_id=1, replica_groups=mesh['slab'=4,'img'=32] {'slab'}, dimensions={1}, use_global_device_ids=true | all-gather | bytes 81920 | tf_op jit(solution)/shard_map/all_gather | solution.py:34
  135.8 11.1 %fusion.33 = bf16[16,64,256]{2,1,0:T(8,128)(2,1)} fusion(bf16[1024,16,64]{0,2,1:T(8,128)(2,1)S(1)} %bitcast.240, f32[16,256,1024]{2,1,0:T(8,128)} %copy-done.3, bf16[256,16,64]{0,2,1:T(8,128)(2,1)} %bitcast.265, bf16[1024,16,64]{0,2,1:T(8,128)(2,1)} %bitcast.263, f32[16,256]{1,0:T(8,128)} %bitcast.271, f32[16,256]{1,0:T(8,128)} %get-tuple-element.21), kind=kOutput, calls=%fused_computation.38 | convolution fusion | flops 1095237632 | bytes 22052864 | tf_op jit(solution)/shard_map/hqk,khd->qhd/dot_general | solution.py:161
  146.9 7.1 %all-gather.5.cloned.1.call-done = bf16[1024,2048]{1,0:T(8,128)(2,1)} async-done(((bf16[256,2048]{1,0:T(8,128)(2,1)}), bf16[1024,2048]{1,0:T(8,128)(2,1)}) %all-gather.5.cloned.1.call-update) | async-done | bytes 4194320 | tf_op jit(solution)/shard_map/all_gather | solution.py:34
  154.0 4.7 %fusion.169 = (bf16[1024,1024]{1,0:T(8,128)(2,1)}, bf16[1024,1024]{1,0:T(8,128)(2,1)}) fusion(bf16[1024,2048]{1,0:T(8,128)(2,1)} %all-gather.5.cloned.1.call-done), kind=kLoop, calls=%fused_computation.211 | loop fusion | bytes 8388608 | tf_op jit(solution)/shard_map/split | solution.py:35
  158.7 2.9 copy.59
  161.6 4.6 %copy.61 = bf16[1024,1024]{0,1:T(8,128)(2,1)} copy(bf16[1024,1024]{1,0:T(8,128)(2,1)} %get-tuple-element.23) | data formatting | bytes 4194304 | tf_op jit(solution)/shard_map/split | solution.py:35
  166.1 3.6 fusion.176
  169.7 4.5 %fusion.35 = bf16[16,64,256]{2,1,0:T(8,128)(2,1)S(1)} fusion(bf16[1024,16,64]{0,2,1:T(8,128)(2,1)S(1)} %bitcast.238, f32[16,1024,256]{2,1,0:T(8,128)S(1)} %fusion.176, f32[16,1024]{1,0:T(8,128)S(1)} %get-tuple-element.42), kind=kOutput, calls=%fused_computation.40 | convolution fusion | flops 549715968 | bytes 19464192 | tf_op jit(solution)/shard_map/hqk,qhd->khd/dot_general | solution.py:186
  174.3 1.2 copy-done.2
  175.5 11.3 %fusion.34 = bf16[16,64,256]{2,1,0:T(8,128)(2,1)} fusion(bf16[1024,16,64]{0,2,1:T(8,128)(2,1)} %bitcast.236, f32[16,1024,256]{2,1,0:T(8,128)} %copy-done.2, bf16[1024,16,64]{0,2,1:T(8,128)(2,1)} %bitcast.237, bf16[256,16,64]{0,2,1:T(8,128)(2,1)S(1)} %bitcast.270, f32[16,1024]{1,0:T(8,128)} %get-tuple-element.41, f32[16,1024]{1,0:T(8,128)S(1)} %get-tuple-element.42), kind=kOutput, calls=%fused_computation.39 | convolution fusion | flops 1095237632 | bytes 22151168 | tf_op jit(solution)/shard_map/hqk,qhd->khd/dot_general | solution.py:183
  186.8 5.2 %fusion.167 = (f32[256]{0:T(256)S(1)}, f32[256]{0:T(256)S(1)}, f32[256,1024]{1,0:T(8,128)S(1)}) fusion(f32[256]{0:T(256)} %copy-done.44, f32[256,1024]{1,0:T(8,128)S(1)} %copy-done.8, f32[256]{0:T(256)} %copy-done.42, f32[1024]{0:T(1024)} %bitcast.273, bf16[1024,3072]{1,0:T(8,128)(2,1)} %param.14, bf16[256,1024]{0,1:T(8,128)(2,1)S(1)} %bitcast.269, ...), kind=kOutput, calls=%fused_computation.209 | convolution fusion | flops 1616903680 | bytes 9969664 | tf_op jit(solution)/shard_map/dot_general | solution.py:65
  194.3 1.8 fusion.61
  202.6 3.1 copy.80
  205.8 3.4 reshape.258
  209.2 2.5 pad_maximum_fusion
  211.8 2.3 collective-permute-start.3
  214.1 4.9 %collective-permute-start.2 = (bf16[1,128,4]{2,1,0:T(8,128)(2,1)S(1)}, bf16[1,128,4]{2,1,0:T(8,128)(2,1)S(1)}, u32[]{:S(2)}, u32[]{:S(2)}) collective-permute-start(bf16[1,128,4]{2,1,0:T(8,128)(2,1)S(1)} %get-tuple-element.39), channel_id=1, source_target_pairs={{0,32},{32,64},{64,96},{1,33},{33,65},{65,97},{2,34},{34,66},{66,9... | collective-permute-start | bytes 3080 | tf_op jit(solution)/shard_map/ppermute | solution.py:22
  223.9 2.1 add_convert_fusion
  226.0 137.4 %all-reduce.4.cloned.1.call-done = f32[804865]{0:T(1024)} async-done(((f32[804865]{0:T(1024)}), f32[804865]{0:T(1024)}) %all-reduce.4.cloned.1.call-update) | async-done | bytes 3219476 | tf_op jit(solution)/shard_map/psum | solution.py:42
  363.4 1.9 slice-done
  365.3 2.0 reshape.260
  367.3 3.8 reshape.261
  371.1 3.0 copy.81
  374.1 1.2 slice.215
  (161 shorter events, 34.6 us)
Async XLA Ops:
  7.2 100.1 %copy-start = (bf16[1024,1024]{1,0:T(8,128)(2,1)S(1)}, bf16[1024,1024]{1,0:T(8,128)(2,1)}, u32[]{:S(2)}) copy-start(bf16[1024,1024]{1,0:T(8,128)(2,1)} %param.15) | copy-start | bytes 6291460
  7.2 73.0 %all-gather.3.cloned.1.call-start = ((), (), s32[]{:S(2)}) async-start(), calls=%async_computation | async-start | bytes 5242880 | tf_op jit(solution)/shard_map/all_gather | solution.py:34
  8.4 11.6 %collective-permute-start = (bf16[1,128,512]{2,1,0:T(8,128)(2,1)S(1)}, bf16[1,128,512]{2,1,0:T(8,128)(2,1)S(1)}, u32[]{:S(2)}, u32[]{:S(2)}) collective-permute-start(bf16[1,128,512]{2,1,0:T(8,128)(2,1)S(1)} %get-tuple-element.37), channel_id=1, source_target_pairs={{0,32},{32,64},{64,96},{1,33},{33,65},{65,97},{2,34},{34,66},{66,9... | collective-permute-start | bytes 393224 | tf_op jit(solution)/shard_map/ppermute | solution.py:22
  14.4 7.8 %collective-permute-start.1 = (bf16[1,128,512]{2,1,0:T(8,128)(2,1)S(1)}, bf16[1,128,512]{2,1,0:T(8,128)(2,1)S(1)}, u32[]{:S(2)}, u32[]{:S(2)}) collective-permute-start(bf16[1,128,512]{2,1,0:T(8,128)(2,1)S(1)} %get-tuple-element.38), channel_id=1, source_target_pairs={{32,0},{64,32},{96,64},{33,1},{65,33},{97,65},{34,2},{66,34},{98,6... | collective-permute-start | bytes 393224 | tf_op jit(solution)/shard_map/ppermute | solution.py:24
  20.0 2.2 copy-start.34
  25.7 1.5 copy-start.32
  25.7 1.6 copy-start.35
  27.5 4.2 %copy-start.39 = (bf16[16,1024]{1,0:T(8,128)(2,1)S(1)}, bf16[16,1024]{1,0:T(8,128)(2,1)}, u32[]{:S(2)}) copy-start(bf16[16,1024]{1,0:T(8,128)(2,1)} %param.12) | copy-start | bytes 98308
  31.7 1.7 copy-start.46
  31.7 1.8 copy-start.47
  33.1 5.1 %copy-start.6 = (f32[256,1024]{1,0:T(8,128)}, f32[256,1024]{1,0:T(8,128)S(1)}, u32[]{:S(2)}) copy-start(f32[256,1024]{1,0:T(8,128)S(1)} %get-tuple-element.47) | copy-start | bytes 3145732
  33.1 5.1 %copy-start.42 = (f32[256]{0:T(256)}, f32[256]{0:T(256)S(1)}, u32[]{:S(2)}) copy-start(f32[256]{0:T(256)S(1)} %broadcast_multiply_fusion.2) | copy-start | bytes 3076
  33.4 4.8 %copy-start.44 = (f32[256]{0:T(256)}, f32[256]{0:T(256)S(1)}, u32[]{:S(2)}) copy-start(f32[256]{0:T(256)S(1)} %add_rsqrt_fusion) | copy-start | bytes 3076
  40.5 113.5 %all-gather.5.cloned.1.call-start = ((), (), s32[]{:S(2)}) async-start(), calls=%async_computation.1 | async-start | bytes 5242880 | tf_op jit(solution)/shard_map/all_gather | solution.py:34
  97.1 6.3 %copy-start.3 = (f32[16,256,1024]{2,1,0:T(8,128)}, f32[16,256,1024]{2,1,0:T(8,128)S(1)}, u32[]{:S(2)}) copy-start(f32[16,256,1024]{2,1,0:T(8,128)S(1)} %get-tuple-element.49) | copy-start | bytes 50331652
  97.1 6.3 %copy-start.23 = (bf16[1024,1024]{0,1:T(8,128)(2,1)S(1)}, bf16[1024,1024]{0,1:T(8,128)(2,1)}, u32[]{:S(2)}) copy-start(bf16[1024,1024]{0,1:T(8,128)(2,1)} %copy.55) | copy-start | bytes 6291460
  103.4 3.8 %copy-start.7 = (f32[256,1024]{1,0:T(8,128)S(1)}, f32[256,1024]{1,0:T(8,128)}, u32[]{:S(2)}) copy-start(f32[256,1024]{1,0:T(8,128)} %copy-done.6) | copy-start | bytes 3145732
  107.2 1.6 copy-start.29
  107.2 1.6 copy-start.36
  108.9 1.6 copy-start.27
  112.9 1.6 copy-start.19
  114.5 2.2 copy-start.24
  115.5 2.1 copy-start.18
  115.5 3.1 copy-start.22
  115.6 247.9 %all-reduce.4.cloned.1.call-start = ((), (), s32[]{:S(2)}) async-start(), calls=%async_computation.2 | async-start | bytes 6447104 | tf_op jit(solution)/shard_map/psum | solution.py:42
  116.6 2.0 copy-start.28
  120.9 14.8 %copy-start.14 = (bf16[1024,1024]{0,1:T(8,128)(2,1)S(1)}, bf16[1024,1024]{0,1:T(8,128)(2,1)}, u32[]{:S(2)}) copy-start(bf16[1024,1024]{0,1:T(8,128)(2,1)} %copy.57) | copy-start | bytes 6291460
  126.9 8.9 %copy-start.41 = (f32[256,16]{0,1:T(8,128)}, f32[256,16]{0,1:T(8,128)S(1)}, u32[]{:S(2)}) copy-start(f32[256,16]{0,1:T(8,128)S(1)} %multiply_reduce_fusion.2) | copy-start | bytes 49156
  161.5 4.6 %copy-start.12 = (bf16[1024,1024]{0,1:T(8,128)(2,1)}, bf16[1024,1024]{0,1:T(8,128)(2,1)S(1)}, u32[]{:S(2)}) copy-start(bf16[1024,1024]{0,1:T(8,128)(2,1)S(1)} %copy.59) | copy-start | bytes 6291460
  166.1 3.6 copy-start.13
  169.7 5.8 %copy-start.2 = (f32[16,1024,256]{2,1,0:T(8,128)}, f32[16,1024,256]{2,1,0:T(8,128)S(1)}, u32[]{:S(2)}) copy-start(f32[16,1024,256]{2,1,0:T(8,128)S(1)} %fusion.176) | copy-start | bytes 50331652
  169.7 5.7 %copy-start.30 = (bf16[256,1024]{0,1:T(8,128)(2,1)S(1)}, bf16[256,1024]{0,1:T(8,128)(2,1)}, u32[]{:S(2)}) copy-start(bf16[256,1024]{0,1:T(8,128)(2,1)} %copy.62) | copy-start | bytes 1572868
  175.5 11.3 %copy-start.8 = (f32[256,1024]{1,0:T(8,128)S(1)}, f32[256,1024]{1,0:T(8,128)}, u32[]{:S(2)}) copy-start(f32[256,1024]{1,0:T(8,128)} %copy-done.6) | copy-start | bytes 3145732
  186.8 5.3 %copy-start.11 = (f32[256,1024]{1,0:T(8,128)S(1)}, f32[256,1024]{1,0:T(8,128)}, u32[]{:S(2)}) copy-start(f32[256,1024]{1,0:T(8,128)} %copy-done.10) | copy-start | bytes 3145732
  186.8 5.3 %copy-start.40 = (bf16[16,1024]{1,0:T(8,128)(2,1)S(1)}, bf16[16,1024]{1,0:T(8,128)(2,1)}, u32[]{:S(2)}) copy-start(bf16[16,1024]{1,0:T(8,128)(2,1)} %param.12) | copy-start | bytes 98308
  186.8 5.3 %copy-start.43 = (f32[256]{0:T(256)S(1)}, f32[256]{0:T(256)}, u32[]{:S(2)}) copy-start(f32[256]{0:T(256)} %copy-done.42) | copy-start | bytes 3076
  186.8 5.3 %copy-start.45 = (f32[256]{0:T(256)S(1)}, f32[256]{0:T(256)}, u32[]{:S(2)}) copy-start(f32[256]{0:T(256)} %copy-done.44) | copy-start | bytes 3076
  192.1 2.2 copy-start.5
  193.4 8.2 %copy-start.15 = (bf16[4,64,2,2,4]{4,3,1,2,0:T(2,128)(2,1)}, bf16[4,64,2,2,4]{4,3,1,2,0:T(2,128)(2,1)S(1)}, u32[]{:S(2)}) copy-start(bf16[4,64,2,2,4]{4,3,1,2,0:T(2,128)(2,1)S(1)} %copy.63) | copy-start | bytes 24580
  198.9 1.9 copy-start.33
  202.6 6.6 %copy-start.9 = (f32[786432]{0:T(1024)S(1)}, f32[786432]{0:T(1024)}, u32[]{:S(2)}) copy-start(f32[786432]{0:T(1024)} %reshape.257) | copy-start | bytes 9437188
  211.7 7.2 %copy-start.16 = (bf16[4,64,2,2,4]{4,3,1,2,0:T(2,128)(2,1)S(1)}, bf16[4,64,2,2,4]{4,3,1,2,0:T(2,128)(2,1)}, u32[]{:S(2)}) copy-start(bf16[4,64,2,2,4]{4,3,1,2,0:T(2,128)(2,1)} %copy-done.15) | copy-start | bytes 24580
  211.7 7.3 %copy-start.38 = (bf16[9,512,4]{1,2,0:T(4,128)(2,1)S(1)}, bf16[9,512,4]{1,2,0:T(4,128)(2,1)}, u32[]{:S(2)}) copy-start(bf16[9,512,4]{1,2,0:T(4,128)(2,1)} %param.11) | copy-start | bytes 110596
  211.8 7.8 %collective-permute-start.3 = (bf16[1,128,4]{2,1,0:T(8,128)(2,1)S(1)}, bf16[1,128,4]{2,1,0:T(8,128)(2,1)S(1)}, u32[]{:S(2)}, u32[]{:S(2)}) collective-permute-start(bf16[1,128,4]{2,1,0:T(8,128)(2,1)S(1)} %get-tuple-element.40), channel_id=1, source_target_pairs={{32,0},{64,32},{96,64},{33,1},{65,33},{97,65},{34,2},{66,34},{98,6... | collective-permute-start | bytes 3080 | tf_op jit(solution)/shard_map/ppermute | solution.py:24
  214.1 6.0 %collective-permute-start.2 = (bf16[1,128,4]{2,1,0:T(8,128)(2,1)S(1)}, bf16[1,128,4]{2,1,0:T(8,128)(2,1)S(1)}, u32[]{:S(2)}, u32[]{:S(2)}) collective-permute-start(bf16[1,128,4]{2,1,0:T(8,128)(2,1)S(1)} %get-tuple-element.39), channel_id=1, source_target_pairs={{0,32},{32,64},{64,96},{1,33},{33,65},{65,97},{2,34},{34,66},{66,9... | collective-permute-start | bytes 3080 | tf_op jit(solution)/shard_map/ppermute | solution.py:22
  363.4 1.9 slice-start
  365.3 2.0 slice-start.1
  367.3 8.7 %copy-start.1 = (bf16[1024,1024]{1,0:T(8,128)(2,1)S(1)}, bf16[1024,1024]{1,0:T(8,128)(2,1)}, u32[]{:S(2)}) copy-start(bf16[1024,1024]{1,0:T(8,128)(2,1)} %param.15) | copy-start | bytes 6291460
  (9 other events, 8.8 us)
Sparse Core Ops, SparseCore 0:
  40.6 39.5 all-gather.2
  115.7 38.2 all-gather.4
  211.9 151.4 all-reduce.3
where the time goes:
time: 389 us; the launch traced here: 384 us
  waiting for transfers between devices  182 us (47%)
  matrix products  75.9 us (20%)
  local copies, waits for them, and re-layouts  71.3 us (18%)
  between operations  17.3 us (4%)
  starting transfers between devices  15.4 us (4%)
  other arithmetic  14.3 us (4%)
  blocking collectives  7.57 us (2%)
    psum x1, waiting for transfers between devices, together(): subtotal = lax.psum(jnp.concatenate([a.ravel() for a in arrays]), axis)  137 us
    all_gather x2, waiting for transfers between devices, sent_together(): out = lax.all_gather(both, axis, axis=dim, tiled=True)  42 us
    split x6, local copies, waits for them, and re-layouts, sent_together(): jnp.split(out, [sum(widths[:k]) for k in range(1, len(widths))], axis=along)  24.8 us
    dot_general x12, matrix products, contract_last(): lax.dot_general(left, right, (((1,), (1,)), ((), ())), preferred_element_...  12.7 us
    unnamed x97, local copies, waits for them, and re-layouts  12.3 us
    dot_general x10, matrix products, contract_first(): lax.dot_general(left, right, (((0,), (0,)), ((), ())), preferred_element_...  11.4 us
    dot_general x1, matrix products, local(): jnp.einsum('hqk,qhd->khd', far_dscores, qa3, preferred_element_type=jnp.f...  11.3 us
    dot_general x1, matrix products, local(): jnp.einsum('hqk,khd->qhd', dscores, k3, preferred_element_type=jnp.float32)  11.1 us
  transfers between devices with their start and end apart: 7, of which 5 were waited for; matrix products, arithmetic and copies ran while one was open for 10% of the time, Pallas kernels for 0%

commit v1 on v0

v1 whole, which is shorter than its diff:
```python
import functools
import jax
import jax.numpy as jnp
from jax import lax
from jax.experimental import pallas as pl
from jax.experimental.pallas import tpu as pltpu
from jax.sharding import Mesh
from jax.sharding import PartitionSpec as P

HEAD_DIM = 64
latent_scale = 0.18215
norm_eps = 1e-06
cosine_eps = 1e-06
LOG2E = 1.4426950408889634
F32 = jnp.float32
BF16 = jnp.bfloat16
INTERPRET = False


def dot(a, b, ca, cb):
    return lax.dot_general(a, b, (((ca,), (cb,)), ((), ())), preferred_element_type=F32)


def split2(x):
    hi = x.astype(BF16)
    lo = (x - hi.astype(F32)).astype(BF16)
    return hi, lo


def split3(x):
    hi = x.astype(BF16)
    r = x - hi.astype(F32)
    mid = r.astype(BF16)
    lo = (r - mid.astype(F32)).astype(BF16)
    return hi, mid, lo


def dot22(a, b, ca, cb):
    ah, al = split2(a)
    bh, bl = split2(b)
    return dot(ah, bh, ca, cb) + dot(ah, bl, ca, cb) + dot(al, bh, ca, cb)


def dot33(a, b, ca, cb):
    ah, am, al = split3(a)
    bh, bm, bl = split3(b)
    small = dot(ah, bl, ca, cb) + dot(al, bh, ca, cb) + dot(am, bm, ca, cb)
    return small + (dot(ah, bm, ca, cb) + dot(am, bh, ca, cb)) + dot(ah, bh, ca, cb)


def iota(shape, axis):
    return lax.broadcasted_iota(jnp.int32, shape, axis)


def call(body, out_shape, in_specs=None, out_specs=None, scratch=(), **kw):
    return pl.pallas_call(
        body,
        out_shape=out_shape,
        in_specs=in_specs,
        out_specs=out_specs,
        scratch_shapes=scratch,
        interpret=INTERPRET,
        compiler_params=pltpu.CompilerParams(vmem_limit_bytes=56 << 20),
        **kw,
    )


def vmem():
    return pl.BlockSpec(memory_space=pltpu.VMEM)


def smem():
    return pl.BlockSpec(memory_space=pltpu.SMEM)


def conv_body(f_ref, w_ref, o_ref):
    y = dot(w_ref[...], f_ref[...], 1, 1)
    tiles = []
    for ky in range(3):
        for h in range(8):
            tiles.append(
                jnp.concatenate(
                    [
                        y[(ky * 3 + kx) * 8 : (ky * 3 + kx) * 8 + 8, h * 128 : h * 128 + 128]
                        for kx in range(3)
                    ],
                    axis=1,
                )
            )
    a = jnp.concatenate(tiles, axis=0)
    row = iota((384, 128), 0)
    col = iota((384, 128), 1)
    w = 2 * (col % 64) + col // 64
    pick = jnp.where(row % 128 == w + row // 128 - 1, 1.0, 0.0).astype(BF16)
    hi, mid, lo = split3(a)
    z = dot(lo, pick, 1, 0) + dot(mid, pick, 1, 0) + dot(hi, pick, 1, 0)

    def latent(r):
        acc = None
        for ky in range(3):
            h = r + ky - 1
            if 0 <= h < 8:
                part = z[(ky * 8 + h) * 8 : (ky * 8 + h) * 8 + 8]
                acc = part if acc is None else acc + part
        return acc

    for i in range(-1, 5):
        parts = []
        if 2 * i >= -1 and 2 * i <= 8:
            parts.append(latent(2 * i))
        if 2 * i + 1 >= -1 and 2 * i + 1 <= 8:
            parts.append(pltpu.roll(latent(2 * i + 1), 4, 0))
        o_ref[(i + 1) * 8 : (i + 2) * 8, :] = sum(parts[1:], parts[0])


def weights_body(lab_ref, e_ref, mod_ref, qkv_ref, outw_ref, m_ref, b_ref, c_ref, ep_ref):
    lab = lab_ref[0]
    rows = mod_ref[...].astype(F32)
    pickrow = iota(rows.shape, 0) == lab % 8
    mod = jnp.sum(jnp.where(pickrow, rows, 0.0), axis=0, keepdims=True)
    shift = mod[:, :1024]
    scale = mod[:, 1024:]
    r = iota((16, 16), 0)
    c = iota((16, 16), 1)
    src = (r // 4 % 2) * 8 + (r // 8) * 4 + r % 4
    perm = jnp.where(c == src, 1.0, 0.0).astype(BF16)
    ef = dot(perm, e_ref[...], 1, 0)
    ep_ref[...] = ef.astype(BF16)
    ec = ef - jnp.mean(ef, axis=1, keepdims=True)
    m_ref[...] = dot33(ec, ec, 1, 1) * (1.0 / 1024)
    hi, mid, lo = split3(ec * (1.0 + scale))
    sh = jnp.where(iota((16, 1024), 0) == 0, shift, 0.0).astype(BF16)
    full = dot(jnp.concatenate([hi, mid, lo, sh], axis=0), qkv_ref[...], 1, 0)
    a = full[:16] + full[16:32] + full[32:48]
    bias = full[48:49]
    aq, ak, av = a[:, :1024], a[:, 1024:2048], a[:, 2048:]
    bq, bk, bv = bias[:, :1024], bias[:, 1024:2048], bias[:, 2048:]
    r16 = iota((16, 1024), 0)
    qexp = jnp.concatenate([aq, jnp.where(r16 == 0, bq, 0.0)], axis=0)
    kexp = jnp.concatenate([ak, ak, ak, jnp.where(r16 < 3, bk, 0.0)], axis=0)
    vexp = jnp.concatenate([av, av, jnp.zeros_like(av), jnp.where(r16 < 3, bv, 0.0)], axis=0)
    even = iota((64, 128), 1) < 64
    for p in range(8):
        s = slice(128 * p, 128 * p + 128)
        k2 = kexp[:, s]
        k4 = jnp.concatenate([jnp.where(even, k2, 0.0), jnp.where(even, 0.0, k2)], axis=0)
        b_ref[:, s] = dot33(qexp[:, s], k4, 1, 1) * (LOG2E / 8.0)
        v2 = vexp[:, s]
        v4 = jnp.concatenate([jnp.where(even, v2, 0.0), jnp.where(even, 0.0, v2)], axis=0)
        hi, lo = split2(v4)
        w = outw_ref[s, :]
        c_ref[s, :] = (dot(hi, w, 1, 0) + dot(lo, w, 1, 0)).astype(BF16)


def lane64(shape):
    return iota(shape, 1) % 64


def with_bias(x, base):
    hi, mid, lo = split3(x)
    col = lane64(x.shape)
    out = jnp.where(col < 48, base.astype(F32), 0.0)
    out = jnp.where(col == 48, hi.astype(F32), out)
    out = jnp.where(col == 49, mid.astype(F32), out)
    out = jnp.where(col == 50, lo.astype(F32), out)
    return out.astype(BF16)


def forward_body(
    s_ref, t0_ref, t1_ref, t2_ref, t3_ref, m_ref, b_ref, c_ref, ep_ref, pw_ref, d_ref,
    gp_ref, gz_ref, w_out, x_out, uk_out, ut_out, vt_out, inv_out, loss_ref,
    tbuf, tok, own, wsel,
):
    s = s_ref[0]
    for k, ref in enumerate((t0_ref, t1_ref, t2_ref, t3_ref)):
        tbuf[(s + 4 - k) % 4] = ref[...]
    left = iota((8, 128), 1) < 64

    def patch_row(t):
        a, i = t // 4, t % 4
        v = tbuf[a, 8 * (i + 1) : 8 * (i + 2), :]
        if i == 3 and a < 3:
            v = v + tbuf[a + 1, 0:8, :]
        if i == 0 and a > 0:
            v = v + tbuf[a - 1, 40:48, :]
        return v * latent_scale

    for j in range(8):
        ta, tb = patch_row(2 * j), patch_row(2 * j + 1)
        tok[0:8, 128 * j : 128 * j + 128] = jnp.where(left, ta, pltpu.roll(tb, 64, 1))
        tok[8:16, 128 * j : 128 * j + 128] = jnp.where(left, pltpu.roll(ta, 64, 1), tb)
    tokt = tok[...]
    v = dot33(m_ref[...], tokt, 1, 0)
    inv = lax.rsqrt(jnp.sum(tokt * v, axis=0, keepdims=True) + norm_eps)
    ut = tokt * inv
    vt = v * inv
    ut_out[...] = ut
    vt_out[...] = vt
    inv_out[...] = jnp.broadcast_to(inv, (8, 1024))
    uh, ul = split2(ut)
    ones = jnp.where(iota((16, 1024), 0) < 3, 1.0, 0.0).astype(BF16)
    uk_out[...] = jnp.concatenate([uh, ul, uh, ones], axis=0)
    for a in range(4):
        own[a, 0:16, :] = tokt[:, 256 * a : 256 * a + 256]
        own[a, 16:32, :] = ut[:, 256 * a : 256 * a + 256]
    mine = own[s]
    tok_own, u_own = mine[0:16], mine[16:32]
    uoh, uol = split2(u_own)
    one16 = jnp.where(iota((16, 256), 0) == 0, 1.0, 0.0).astype(BF16)
    zero16 = jnp.zeros((16, 256), BF16)
    lhs = jnp.concatenate([uoh, one16, uoh, one16, uol, zero16], axis=0)
    bh, bl = split2(b_ref[...])
    wall = dot(lhs, jnp.concatenate([bh, bl, bh], axis=0), 0, 0)
    hi = wall.astype(BF16)
    rest = (wall - hi.astype(F32)).astype(BF16)
    base = jnp.where(lane64(wall.shape) < 32, hi.astype(F32), rest.astype(F32))
    sel = with_bias(wall, base)
    for p in range(8):
        wsel[p] = sel[:, 128 * p : 128 * p + 128]
        w_out[p] = wall[:, 128 * p : 128 * p + 128]
    zk = jnp.zeros((64, 1024), BF16)
    uk = uk_out[...]
    uke = jnp.concatenate([uk, zk], axis=0)
    uko = jnp.concatenate([zk, uk], axis=0)
    lane = iota((256, 128), 1)

    def pair(p, carry):
        w = wsel[p]
        x = None
        tops = []
        for u in (uke, uko):
            sc = dot(w, u, 1, 0)
            top = jnp.max(sc, axis=1, keepdims=True)
            e = jnp.exp2(sc - top).astype(BF16)
            part = dot(e, u, 1, 1)
            x = part if x is None else x + part
            tops.append(top)
        t0, t1 = x[:, 48:49], x[:, 112:113]
        total = jnp.where(lane < 64, t0, t1)
        top = jnp.where(lane < 64, tops[0], tops[1])
        lse = top + jnp.log2(total)
        x_out[p] = jnp.where(lane % 64 < 49, x / total, 0.0).astype(BF16)
        w_out[p] = jnp.where(lane % 64 >= 48, w_out[p] - lse, w_out[p])
        return carry

    lax.fori_loop(0, 8, pair, 0)
    xn = jnp.concatenate([x_out[p] for p in range(8)], axis=1)
    th, tm, tl = split3(tok_own)
    ep = ep_ref[...]
    start = dot(jnp.concatenate([th, tm, tl], axis=0), jnp.concatenate([ep, ep, ep], axis=0), 0, 0)
    resid = start + dot(xn, c_ref[...], 1, 0)
    rb = resid.astype(BF16)
    zp = dot(rb, pw_ref[...], 1, 0)
    d = d_ref[...].astype(F32)
    nz2 = jnp.sum(zp * zp, axis=1, keepdims=True) + cosine_eps
    nd2 = jnp.sum(d * d, axis=1, keepdims=True) + cosine_eps
    zd = jnp.sum(zp * d, axis=1, keepdims=True)
    both = lax.rsqrt(nz2) * lax.rsqrt(nd2)
    cosine = zd * both
    gz = ((cosine / nz2) * zp - both * d).astype(BF16)
    gz_ref[...] = gz
    loss_ref[...] = jnp.broadcast_to(jnp.sum(1.0 - cosine, axis=0, keepdims=True), (8, 128))
    gp_ref[...] = dot(rb, gz, 0, 0).astype(gp_ref.dtype)


def backward_body(
    s_ref, gz_ref, w_ref, x_ref, uk_ref, ut_ref, vt_ref, inv_ref, b_ref, c_ref, ep_ref, pw_ref,
    o_ref,
    wsel, gsel, wt, gt, ysc, hk, hv, padded,
):
    s = s_ref[0]
    gresid = dot(gz_ref[...], pw_ref[...], 1, 1)
    gh, gl = split2(gresid)
    ep = ep_ref[...]
    r_own = dot(ep, gh, 1, 1) + dot(ep, gl, 1, 1)
    gexp = dot(gh, c_ref[...], 1, 1)
    r128 = iota((128, 128), 0) // 64
    c128 = iota((128, 128), 1) // 64
    block = jnp.where(r128 == c128, 1.0, 0.0).astype(BF16)
    col = iota((256, 128), 1) % 64
    for p in range(8):
        g = gexp[:, 128 * p : 128 * p + 128]
        g_hi = g.astype(BF16).astype(F32)
        ph, plo = split2(g_hi * x_ref[p].astype(F32))
        delta = dot(ph, block, 1, 0) + dot(plo, block, 1, 0)
        gs = with_bias(g_hi - delta, jnp.where(col < 32, g_hi, 0.0))
        gsel[p] = gs
        gt[p] = gs.astype(F32).T.astype(BF16)
        w = w_ref[p]
        hi = w.astype(BF16).astype(F32)
        ws = with_bias(w, jnp.where(col < 32, hi, w - hi))
        wsel[p] = ws
        wt[p] = ws.astype(F32).T.astype(BF16)
    hk[...] = jnp.zeros_like(hk)
    hv[...] = jnp.zeros_like(hv)
    uk = uk_ref[...]
    zk = jnp.zeros((64, 1024), BF16)
    uke = jnp.concatenate([uk, zk], axis=0)
    uko = jnp.concatenate([zk, uk], axis=0)

    def pair(p, carry):
        w = wsel[p]
        g = gsel[p]
        y = None
        for half, u in enumerate((uke, uko)):
            prob = jnp.exp2(dot(w, u, 1, 0))
            ds = (prob * dot(g, u, 1, 0)).astype(BF16)
            pb = prob.astype(BF16)
            part = dot(ds, u, 1, 1)
            y = part if y is None else y + part
            hk[...] += dot(wt[p, 64 * half : 64 * half + 16, :], ds, 1, 0)
            hv[...] += dot(gt[p, 64 * half : 64 * half + 16, :], pb, 1, 0)
        ysc[p] = jnp.where((col < 32) | (col == 48), y, 0.0)
        return carry

    lax.fori_loop(0, 8, pair, 0)
    y = jnp.concatenate([ysc[p] for p in range(8)], axis=1)
    ln2 = 1.0 / LOG2E
    hq = dot22(b_ref[...], y, 1, 1)[0:16] * ln2
    h = hk[...] * ln2 + hv[...]
    own = padded
    for a in range(4):
        mineq = jnp.where(s == a, 1.0, 0.0)
        own[a, :, 0:256] = h[:, 256 * a : 256 * a + 256] + mineq * hq
    h = jnp.concatenate([own[a, :, 0:256] for a in range(4)], axis=1)
    ut = ut_ref[...]
    inv = inv_ref[0:1, :]
    g = inv * (h - vt_ref[...] * jnp.sum(ut * h, axis=0, keepdims=True))
    z = jnp.zeros((16, 128), F32)
    pieces = []
    for a in range(4):
        mineq = jnp.where(s == a, 1.0, 0.0)
        pieces.append((g[:, 256 * a : 256 * a + 256] + mineq * r_own) * latent_scale)
    line = jnp.concatenate([z] + pieces + [z], axis=1)
    for a in range(4):
        padded[a] = line[:, 256 * a : 256 * a + 512]
    for k in range(4):
        o_ref[k] = padded[(s + k) % 4]


def output_body(g0_ref, g1_ref, g2_ref, g3_ref, f_ref, w_ref, o_ref, gc_ref):
    g = (g0_ref[...] + g1_ref[...] + g2_ref[...] + g3_ref[...]).astype(BF16).astype(F32)
    left = iota((8, 128), 1) < 64
    tiles = []
    for j in range(4):
        x0 = g[0:8, 128 * j : 128 * j + 128]
        x1 = g[8:16, 128 * j : 128 * j + 128]
        tiles.append(jnp.where(left, x0, pltpu.roll(x1, 64, 1)))
        tiles.append(jnp.where(left, pltpu.roll(x0, 64, 1), x1))
    t = jnp.concatenate(tiles[1:7], axis=0).astype(BF16)
    q = iota((128, 384), 0)
    col = iota((128, 384), 1)
    pick = jnp.where(2 * (q % 64) + q // 64 == col % 128 + 1 - col // 128, 1.0, 0.0).astype(BF16)
    v = dot(t, pick, 1, 0)

    def tile(i, kx):
        return v[8 * (i + 1) : 8 * (i + 2), 128 * kx : 128 * kx + 128]

    acc = [None, None]
    for a in range(8):
        i = a // 2
        other = i - 1 if a % 2 == 0 else i + 1
        rows = []
        for kx in range(3):
            rows += [tile(i, kx), tile(other, kx)]
        gt = jnp.concatenate(rows, axis=0).astype(BF16)
        o_ref[128 * a : 128 * a + 128, :] = dot(gt, w_ref[a % 2], 0, 0).astype(BF16)
        part = dot(gt, f_ref[128 * a : 128 * a + 128, :], 1, 0)
        acc[a % 2] = part if acc[a % 2] is None else acc[a % 2] + part
    ev, od = acc
    for kx in range(3):
        et, epv = ev[16 * kx : 16 * kx + 8], ev[16 * kx + 8 : 16 * kx + 16]
        ot, on = od[16 * kx : 16 * kx + 8], od[16 * kx + 8 : 16 * kx + 16]
        gc_ref[kx] = pltpu.roll(et, 4, 0) + on
        gc_ref[3 + kx] = et + pltpu.roll(ot, 4, 0)
        gc_ref[6 + kx] = pltpu.roll(epv, 4, 0) + ot


def shifted(x, axis, n, k):
    return lax.ppermute(x, axis, [(i, (i + k) % n) for i in range(n)])


SLAB = ("xh", "core")
CHIPS = ("xh", "z", "y", "xl")


def reduced(parts):
    n = parts.shape[-1]
    core = lax.axis_index("core")
    halves = parts.reshape(2, 64, 8, n)
    mine = lax.dynamic_index_in_dim(halves, core, 0, keepdims=False)
    other = lax.dynamic_index_in_dim(halves, 1 - core, 0, keepdims=False)
    got = shifted(other, "core", 2, 1)
    chip = (mine.astype(F32) + got.astype(F32)).astype(BF16)
    pieces = lax.all_to_all(chip, CHIPS, split_axis=0, concat_axis=0, tiled=True)
    return jnp.sum(pieces.astype(F32), 0)


def gathered(block):
    n = block.shape[-1]
    same = jnp.broadcast_to(block[None], (64, 8, n))
    half = lax.all_to_all(same, CHIPS, split_axis=0, concat_axis=0, tiled=True)
    other = shifted(half, "core", 2, 1)
    core = lax.axis_index("core")
    return jnp.where(core == 0, half, other), jnp.where(core == 0, other, half)


def local(feats, labels, conv_w, embed_w, mod_table, qkv_w, out_w, proj_w, dino):
    slab = (lax.axis_index("xh") * 2 + lax.axis_index("core")).astype(jnp.int32).reshape(1)
    image = feats.reshape(1024, 512)
    taps = conv_w.transpose(0, 2, 1)
    w72 = jnp.pad(taps, ((0, 0), (0, 4), (0, 0))).reshape(72, 512)
    t3 = taps.reshape(3, 3, 4, 512)
    none = jnp.zeros_like(t3[0])
    w_even = jnp.stack([t3[1], t3[0], none, t3[2]], axis=1).reshape(48, 512)
    w_odd = jnp.stack([t3[2], t3[1], t3[0], none], axis=1).reshape(48, 512)
    w_back = jnp.stack([w_even, w_odd])

    part = call(
        conv_body, jax.ShapeDtypeStruct((48, 128), F32), [vmem(), vmem()], vmem()
    )(image, w72)
    parts = [part] + [shifted(part, SLAB, 4, k) for k in (1, 2, 3)]

    mat, bexp, cexp, ep = pl.pallas_call(
        weights_body,
        out_shape=(
            jax.ShapeDtypeStruct((16, 16), F32),
            jax.ShapeDtypeStruct((32, 1024), F32),
            jax.ShapeDtypeStruct((1024, 1024), BF16),
            jax.ShapeDtypeStruct((16, 1024), BF16),
        ),
        grid_spec=pltpu.PrefetchScalarGridSpec(
            num_scalar_prefetch=1,
            grid=(1,),
            in_specs=[
                pl.BlockSpec((16, 1024), lambda i, lab: (0, 0)),
                pl.BlockSpec((8, 2048), lambda i, lab: (lab[0] // 8, 0)),
                pl.BlockSpec((1024, 3072), lambda i, lab: (0, 0)),
                pl.BlockSpec((1024, 1024), lambda i, lab: (0, 0)),
            ],
            out_specs=[
                pl.BlockSpec((16, 16), lambda i, lab: (0, 0)),
                pl.BlockSpec((32, 1024), lambda i, lab: (0, 0)),
                pl.BlockSpec((1024, 1024), lambda i, lab: (0, 0)),
                pl.BlockSpec((16, 1024), lambda i, lab: (0, 0)),
            ],
        ),
        interpret=INTERPRET,
        compiler_params=pltpu.CompilerParams(vmem_limit_bytes=56 << 20),
    )(labels, embed_w, mod_table, qkv_w, out_w)

    gp, gz, w_all, x_all, uk, ut, vt, inv, loss = call(
        forward_body,
        (
            jax.ShapeDtypeStruct((1024, 768), BF16),
            jax.ShapeDtypeStruct((256, 768), BF16),
            jax.ShapeDtypeStruct((8, 256, 128), F32),
            jax.ShapeDtypeStruct((8, 256, 128), BF16),
            jax.ShapeDtypeStruct((64, 1024), BF16),
            jax.ShapeDtypeStruct((16, 1024), F32),
            jax.ShapeDtypeStruct((16, 1024), F32),
            jax.ShapeDtypeStruct((8, 1024), F32),
            jax.ShapeDtypeStruct((8, 128), F32),
        ),
        [smem()] + [vmem()] * 10,
        tuple([vmem()] * 9),
        scratch=[
            pltpu.VMEM((4, 48, 128), F32),
            pltpu.VMEM((16, 1024), F32),
            pltpu.VMEM((4, 32, 256), F32),
            pltpu.VMEM((8, 256, 128), BF16),
        ],
    )(slab, *parts, mat, bexp, cexp, ep, proj_w, dino.reshape(256, 768))

    pieces = call(
        backward_body,
        jax.ShapeDtypeStruct((4, 16, 512), F32),
        [smem()] + [vmem()] * 11,
        vmem(),
        scratch=[
            pltpu.VMEM((8, 256, 128), BF16),
            pltpu.VMEM((8, 256, 128), BF16),
            pltpu.VMEM((8, 128, 256), BF16),
            pltpu.VMEM((8, 128, 256), BF16),
            pltpu.VMEM((8, 256, 128), F32),
            pltpu.VMEM((16, 1024), F32),
            pltpu.VMEM((16, 1024), F32),
            pltpu.VMEM((4, 16, 512), F32),
        ],
    )(slab, gz, w_all, x_all, uk, ut, vt, inv, bexp, cexp, ep, proj_w)
    grads = [pieces[0]] + [shifted(pieces[k], SLAB, 4, k) for k in (1, 2, 3)]

    grad_image, gconv = call(
        output_body,
        (jax.ShapeDtypeStruct((1024, 512), BF16), jax.ShapeDtypeStruct((9, 8, 512), F32)),
        [vmem()] * 6,
        (vmem(), vmem()),
    )(*grads, image, w_back)

    conv_part = gconv.astype(BF16).reshape(9, 8, 4, 128).transpose(0, 2, 1, 3).reshape(36, 8, 128)
    total = loss[0, 0]
    lh, lm, ll = split3(total)
    lane = jnp.arange(128)
    loss_row = jnp.where(lane == 0, lh, jnp.where(lane == 1, lm, jnp.where(lane == 2, ll, 0)))
    loss_part = jnp.broadcast_to(loss_row.astype(BF16), (1, 8, 128))
    extra = jnp.concatenate([conv_part, loss_part, jnp.zeros((91, 8, 128), BF16)])
    both = jnp.concatenate([gp.reshape(128, 8, 768), extra], axis=2)
    block = reduced(both)
    lsum = jnp.sum(block[0, 768:771])
    lh, lm, ll = split3(lsum)
    pos = (lax.axis_index(CHIPS) + 64 * lax.axis_index("core")) == 36
    wide = jnp.arange(896)[None, :]
    coded = jnp.where(wide == 768, lh, jnp.where(wide == 769, lm, ll)).astype(BF16)
    is_loss = pos & (wide >= 768) & (wide < 771)
    block = jnp.where(is_loss, coded, block.astype(BF16))
    first, second = gathered(block)
    grad_proj = jnp.concatenate([first[:, :, :768], second[:, :, :768]]).reshape(1024, 768).astype(F32)
    conv = first[:36, :4, 768:].astype(F32).reshape(9, 4, 4, 128).transpose(0, 2, 1, 3)
    grad_conv = conv.reshape(9, 4, 512).transpose(0, 2, 1)
    loss_sum = jnp.sum(first[36, 0, 768:771].astype(F32))
    return (
        grad_image.reshape(1, 8, 128, 512),
        grad_proj,
        grad_conv,
        loss_sum / 32768.0,
    )


def solution(mesh):
    fine = Mesh(mesh.devices.reshape(2, 2, 4, 4, 2), ("xh", "core", "z", "y", "xl"))
    img = ("z", "y", "xl")
    in_specs = (
        P(img, SLAB, None, None), P(img), P(), P(), P(), P(), P(), P(), P(img, SLAB, None),
    )
    out_specs = (P(img, SLAB, None, None), P(), P(), P())
    return jax.shard_map(local, mesh=fine, in_specs=in_specs, out_specs=out_specs, check_vma=False)
```

time: 389 us -> 140 us (0.36); the launches traced: 384 us -> 140 us
  waiting for transfers between devices: 182 us -> 20.8 us
  matrix products: 75.9 us -> 0 us
  local copies, waits for them, and re-layouts: 71.3 us -> 6.45 us
  Pallas kernels: 0 us -> 51.4 us
  blocking collectives: 7.57 us -> 19.9 us
  starting transfers between devices: 15.4 us -> 26.9 us
  between operations: 17.3 us -> 5.88 us
  other arithmetic: 14.3 us -> 8.33 us
    psum x1 -> x0, waiting for transfers between devices: 137 us -> none  [together(): subtotal = lax.psum(jnp.concatenate([a.ravel() for a in arrays]), axis)]
    dot_general x42 -> x0, matrix products: 75.9 us -> none  [the longest x12 12.7 us: contract_last(): lax.dot_general(left, right, (((1,), (1,)), ((), ())), preferred_element_...]
    pallas_call x0 -> x5, Pallas kernels: none -> 51.4 us  [the longest x1 20.4 us: local(): call(backward_body, jax.ShapeDtypeStruct((4, 16, 512), F32), [smem()] + [...]
    all_gather x2 -> x0, waiting for transfers between devices: 42 us -> none  [sent_together(): out = lax.all_gather(both, axis, axis=dim, tiled=True)]
    split x6 -> x0, local copies, waits for them, and re-layouts: 24.8 us -> none  [sent_together(): jnp.split(out, [sum(widths[:k]) for k in range(1, len(widths))], axis=along)]
    all_to_all x0 -> x1, blocking collectives: none -> 19.9 us  [gathered(): half = lax.all_to_all(same, CHIPS, split_axis=0, concat_axis=0, tiled=True)]
    all_to_all x0 -> x1, waiting for transfers between devices: none -> 15.2 us  [reduced(): lax.all_to_all(chip, CHIPS, split_axis=0, concat_axis=0, tiled=True)]
    reshape x5 -> x1, local copies, waits for them, and re-layouts: 14.5 us -> 1.42 us  [local(): w72 = jnp.pad(taps, ((0, 0), (0, 4), (0, 0))).reshape(72, 512)]
  transfers between devices with their start and end apart: 7 -> 9, of which waited for: 5 -> 5; matrix products, arithmetic and copies ran while one was open for 10% -> 1% of each run, Pallas kernels for 0% -> 6%
where the time goes in v1:
time: 140 us
  Pallas kernels  51.4 us (37%)
  starting transfers between devices  26.9 us (19%)
  waiting for transfers between devices  20.8 us (15%)
  blocking collectives  19.9 us (14%)
  other arithmetic  8.33 us (6%)
  local copies, waits for them, and re-layouts  6.45 us (5%)
  between operations  5.88 us (4%)
    pallas_call x1, Pallas kernels, local(): call(backward_body, jax.ShapeDtypeStruct((4, 16, 512), F32), [smem()] + [...  20.4 us
    all_to_all x1, blocking collectives, gathered(): half = lax.all_to_all(same, CHIPS, split_axis=0, concat_axis=0, tiled=True)  19.9 us
    ppermute x8, starting transfers between devices, shifted(): return lax.ppermute(x, axis, [(i, (i + k) % n) for i in range(n)])  17.7 us
    pallas_call x1, Pallas kernels, local(): call(forward_body, (jax.ShapeDtypeStruct((1024, 768), BF16), jax.ShapeDty...  17.4 us
    all_to_all x1, waiting for transfers between devices, reduced(): lax.all_to_all(chip, CHIPS, split_axis=0, concat_axis=0, tiled=True)  15.2 us
    all_to_all x1, starting transfers between devices, reduced(): lax.all_to_all(chip, CHIPS, split_axis=0, concat_axis=0, tiled=True)  9.26 us
    pallas_call x1, Pallas kernels, local(): pl.pallas_call(weights_body, out_shape=(jax.ShapeDtypeStruct((16, 16), F3...  8.03 us
    ppermute x8, waiting for transfers between devices, shifted(): return lax.ppermute(x, axis, [(i, (i + k) % n) for i in range(n)])  5.53 us
  transfers between devices with their start and end apart: 9, of which 5 were waited for; matrix products, arithmetic and copies ran while one was open for 1% of the time, Pallas kernels for 6%

profile of v1, /device:TPU:1, one launch (start us, length us, event | category | flops | bytes accessed | tf_op | source)
XLA Modules:
  0.0 139.6 jit_solution(12785385702682300125)
XLA Ops:
  0.6 1.4 %pad_bitcast_fusion.w_ref = bf16[72,512]{1,0:T(8,128)(2,1)} fusion(bf16[9,4,512]{2,1,0:T(4,128)(2,1)} %bitcast.53), kind=kLoop, calls=%fused_computation.19 | loop fusion | bytes 110592 | tf_op jit(solution)/shard_map/reshape | solution.py:412
  2.0 2.5 %shard_map.120.t0_ref = f32[48,128]{1,0:T(8,128)} custom-call(bf16[1024,512]{1,0:T(8,128)(2,1)} %bitcast.47, bf16[72,512]{1,0:T(8,128)(2,1)} %pad_bitcast_fusion.w_ref), custom_call_target="tpu_custom_call" | custom-call | tf_op jit(solution)/shard_map/pallas_call | solution.py:419
  4.5 1.4 collective-permute-start.2
  5.9 2.9 %collective-permute-start.1 = (f32[48,128]{1,0:T(8,128)}, f32[48,128]{1,0:T(8,128)S(1)}, u32[]{:S(2)}, u32[]{:S(2)}) collective-permute-start(f32[48,128]{1,0:T(8,128)} %shard_map.120.t0_ref), channel_id=1, source_target_pairs={{0,64},{32,96},{64,0},{96,32},{1,65},{33,97},{65,1},{97,33},{2,66}... | collective-permute-start | bytes 73736 | tf_op jit(solution)/shard_map/ppermute | solution.py:380
  8.8 2.9 %collective-permute-start = (f32[48,128]{1,0:T(8,128)}, f32[48,128]{1,0:T(8,128)S(1)}, u32[]{:S(2)}, u32[]{:S(2)}) collective-permute-start(f32[48,128]{1,0:T(8,128)} %shard_map.120.t0_ref), channel_id=1, source_target_pairs={{0,32},{32,64},{64,96},{96,0},{1,33},{33,65},{65,97},{97,1},{2,34}... | collective-permute-start | bytes 73736 | tf_op jit(solution)/shard_map/ppermute | solution.py:380
  11.6 0.8 slice_bitcast_fusion.4
  12.4 0.1 pad_maximum_fusion.2
  12.6 0.6 pad_maximum_fusion.w_ref
  13.9 0.1 pad.11.clone
  14.0 8.0 %shard_map.121 = (f32[16,16]{1,0:T(8,128)}, f32[32,1024]{1,0:T(8,128)}, bf16[1024,1024]{1,0:T(8,128)(2,1)}, bf16[16,1024]{1,0:T(8,128)(2,1)}) custom-call(s32[1]{0:T(128)S(6)} %copy.17.lab_ref, bf16[16,1024]{1,0:T(8,128)(2,1)} %e_ref.1, bf16[1000,2048]{1,0:T(8,128)(2,1)} %mod_ref.1, bf16[1024,3072]{1,0:T(8,128)(2,1)} %qkv_ref.1, bf16[1024,1024]{1,0:T(8,128)(2,1)} %outw_ref.1), custom_call_target="tpu_custom_call" | custom-call | tf_op jit(solution)/shard_map/pallas_call | solution.py:424
  22.0 0.0 collective-permute-done.2.t3_ref
  22.0 0.0 collective-permute-done.1.t2_ref
  22.0 0.6 copy-done.4
  22.6 0.0 copy-done.5
  22.6 0.0 copy-done.6
  22.6 17.4 %shard_map.122 = (bf16[1024,768]{1,0:T(8,128)(2,1)}, bf16[256,768]{1,0:T(8,128)(2,1)}, f32[8,256,128]{2,1,0:T(8,128)}, bf16[8,256,128]{2,1,0:T(8,128)(2,1)}, bf1...) custom-call(s32[1]{0:T(128)} %bitcast.s_ref, ...), custom_call_target="tpu_custom_call" | custom-call | tf_op jit(solution)/shard_map/pallas_call | solution.py:452
  40.0 1.2 slice.68
  42.5 20.4 %shard_map.123 = f32[4,16,512]{2,1,0:T(8,128)} custom-call(s32[1]{0:T(128)} %bitcast.s_ref, bf16[256,768]{1,0:T(8,128)(2,1)} %get-tuple-element.23.gz_ref, f32[8,256,128]{2,1,0:T(8,128)} %get-tuple-element.24.w_ref, bf16[8,256,128]{2,1,0:T(8,128)(2,1)} %get-tuple-element.25.x_ref, bf16[64,1024]{1,0:T(8,128)(2,1)} %get-tuple-element.26.uk_ref, ...), custom_call_target="tpu_custom_call" | custom-call | tf_op jit(solution)/shard_map/pallas_call | solution.py:475
  62.9 1.5 %slice_bitcast_fusion = (f32[16,512]{1,0:T(8,128)S(1)}, f32[16,512]{1,0:T(8,128)S(1)}, f32[16,512]{1,0:T(8,128)S(1)}, f32[16,512]{1,0:T(8,128)}) fusion(f32[4,16,512]{2,1,0:T(8,128)} %shard_map.123), kind=kLoop, calls=%fused_computation.22 | loop fusion | bytes 262144 | tf_op jit(solution)/shard_map/squeeze | solution.py:491
  64.4 0.3 collective-permute-start.4
  64.7 3.5 %collective-permute-start.3 = (f32[16,512]{1,0:T(8,128)S(1)}, f32[16,512]{1,0:T(8,128)S(1)}, u32[]{:S(2)}, u32[]{:S(2)}) collective-permute-start(f32[16,512]{1,0:T(8,128)S(1)} %get-tuple-element.36), channel_id=1, source_target_pairs={{0,32},{32,64},{64,96},{96,0},{1,33},{33,65},{65,97},{97,1},{2,34}... | collective-permute-start | bytes 98312 | tf_op jit(solution)/shard_map/ppermute | solution.py:380
  68.3 1.0 collective-permute-done.5.g3_ref
  69.3 0.0 collective-permute-done.4.g2_ref
  69.3 0.2 collective-permute-done.3.g1_ref
  69.5 0.4 copy-done.1
  69.9 0.0 copy-done.2
  69.9 0.2 copy-done.3
  70.0 3.1 %shard_map.124 = (bf16[1024,512]{1,0:T(8,128)(2,1)}, f32[9,8,512]{2,1,0:T(8,128)}) custom-call(f32[16,512]{1,0:T(8,128)} %get-tuple-element.37.g0_ref, f32[16,512]{1,0:T(8,128)} %copy-done.3, f32[16,512]{1,0:T(8,128)} %copy-done.2, f32[16,512]{1,0:T(8,128)} %copy-done.1, bf16[1024,512]{1,0:T(8,128)(2,1)} %bitcast.48, bf16[2,48,512]{2,1,0:T(8,128)(2,1)} %pad_maximum_fusion.w_ref), custom_call_target="tpu_custom_call" | custom-call | tf_op jit(solution)/shard_map/pallas_call | solution.py:493
  73.1 0.9 convert_element_type.70
  74.1 0.2 maximum_maximum_fusion
  74.3 0.1 fusion.3
  74.4 3.5 %collective-permute-start.6 = (bf16[64,8,896]{2,1,0:T(8,128)(2,1)S(1)}, bf16[64,8,896]{2,1,0:T(8,128)(2,1)}, u32[]{:S(2)}, u32[]{:S(2)}) collective-permute-start(bf16[64,8,896]{2,1,0:T(8,128)(2,1)S(1)} %fusion.3), channel_id=1, source_target_pairs={{0,32},{32,0},{1,33},{33,1},{2,34},{34,2},{3,35},{35,3},{4,36},{36... | collective-permute-start | bytes 2752520 | tf_op jit(solution)/shard_map/ppermute | solution.py:380
  78.0 2.2 %collective-permute-done.6 = bf16[64,8,896]{2,1,0:T(8,128)(2,1)} collective-permute-done((bf16[64,8,896]{2,1,0:T(8,128)(2,1)S(1)}, bf16[64,8,896]{2,1,0:T(8,128)(2,1)}, u32[]{:S(2)}, u32[]{:S(2)}) %collective-permute-start.6) | collective-permute-done | bytes 917536 | tf_op jit(solution)/shard_map/ppermute | solution.py:380
  80.2 2.3 %fusion = bf16[64,8,896]{2,1,0:T(8,128)(2,1)} fusion(bf16[64,8,896]{2,1,0:T(8,128)(2,1)} %collective-permute-done.6, s32[]{:T(128)S(6)} %select_n.60, bf16[2,64,8,768]{3,2,1,0:T(8,128)(2,1)S(1)} %bitcast.46, bf16[2,64,8,128]{3,2,1,0:T(8,128)(2,1)S(1)} %bitcast.50), kind=kLoop, calls=%fused_computation.3 | loop fusion | flops 3670016 | bytes 3670020 | tf_op jit(solution)/shard_map/convert_element_type | solution.py:394
  82.5 9.3 %all-to-all-start = ((bf16[64,8,896]{2,1,0:T(8,128)(2,1)}), bf16[64,8,896]{2,1,0:T(8,128)(2,1)S(1)}, u32[]{:S(2)}, u32[]{:S(2)}) async-start(bf16[64,8,896]{2,1,0:T(8,128)(2,1)} %fusion), calls=%async_computation | async-start | bytes 1835008 | tf_op jit(solution)/shard_map/all_to_all | solution.py:395
  91.8 15.2 %all-to-all-done = bf16[64,8,896]{2,1,0:T(8,128)(2,1)S(1)} async-done(((bf16[64,8,896]{2,1,0:T(8,128)(2,1)}), bf16[64,8,896]{2,1,0:T(8,128)(2,1)S(1)}, u32[]{:S(2)}, u32[]{:S(2)}) %all-to-all-start) | async-done | bytes 917536 | tf_op jit(solution)/shard_map/all_to_all | solution.py:395
  107.0 0.2 convert_reduce_fusion
  107.2 0.6 slice_reduce_fusion
  109.1 0.1 broadcast_in_dim.67
  109.2 19.9 %all_to_all.10 = bf16[64,8,896]{2,1,0:T(8,128)(2,1)S(1)} all-to-all(bf16[64,8,896]{2,1,0:T(8,128)(2,1)S(1)} %broadcast_in_dim.67), channel_id=1, replica_groups=mesh['xh'=2,'core'=2,'z'=4,'y'=4,'xl'=2] {'xh','z','y','xl'}, dimensions={0} | all-to-all | bytes 1835008 | tf_op jit(solution)/shard_map/all_to_all | solution.py:402
  129.1 3.2 %collective-permute-start.7 = (bf16[64,8,896]{2,1,0:T(8,128)(2,1)S(1)}, bf16[64,8,896]{2,1,0:T(8,128)(2,1)S(1)}, u32[]{:S(2)}, u32[]{:S(2)}) collective-permute-start(bf16[64,8,896]{2,1,0:T(8,128)(2,1)S(1)} %all_to_all.10), channel_id=1, source_target_pairs={{0,32},{32,0},{1,33},{33,1},{2,34},{34,2},{3,35},{35,3},{4,36},{36... | collective-permute-start | bytes 2752520 | tf_op jit(solution)/shard_map/ppermute | solution.py:380
  132.4 2.1 %collective-permute-done.7 = bf16[64,8,896]{2,1,0:T(8,128)(2,1)S(1)} collective-permute-done((bf16[64,8,896]{2,1,0:T(8,128)(2,1)S(1)}, bf16[64,8,896]{2,1,0:T(8,128)(2,1)S(1)}, u32[]{:S(2)}, u32[]{:S(2)}) %collective-permute-start.7) | collective-permute-done | bytes 917536 | tf_op jit(solution)/shard_map/ppermute | solution.py:380
  134.5 0.1 broadcast_select_fusion
  134.6 0.6 fusion.10
  135.2 0.1 slice.86
  135.3 0.6 convert_bitcast_fusion
  136.5 0.1 slice_select_fusion
  136.6 1.9 %fusion.1 = f32[1024,768]{1,0:T(8,128)} fusion(bf16[64,8,768]{2,1,0:T(8,128)(2,1)S(1)} %slice_select_fusion, bf16[64,8,768]{2,1,0:T(8,128)(2,1)S(1)} %slice.86), kind=kLoop, calls=%fused_computation.8 | loop fusion | flops 1572864 | bytes 4718592 | tf_op jit(solution)/shard_map/convert_element_type | solution.py:517
  (24 shorter events, 0.2 us)
Async XLA Ops:
  4.5 17.4 %collective-permute-start.2 = (f32[48,128]{1,0:T(8,128)}, f32[48,128]{1,0:T(8,128)S(1)}, u32[]{:S(2)}, u32[]{:S(2)}) collective-permute-start(f32[48,128]{1,0:T(8,128)} %shard_map.120.t0_ref), channel_id=1, source_target_pairs={{0,96},{32,0},{64,32},{96,64},{1,97},{33,1},{65,33},{97,65},{2,98}... | collective-permute-start | bytes 73736 | tf_op jit(solution)/shard_map/ppermute | solution.py:380
  5.9 16.1 %collective-permute-start.1 = (f32[48,128]{1,0:T(8,128)}, f32[48,128]{1,0:T(8,128)S(1)}, u32[]{:S(2)}, u32[]{:S(2)}) collective-permute-start(f32[48,128]{1,0:T(8,128)} %shard_map.120.t0_ref), channel_id=1, source_target_pairs={{0,64},{32,96},{64,0},{96,32},{1,65},{33,97},{65,1},{97,33},{2,66}... | collective-permute-start | bytes 73736 | tf_op jit(solution)/shard_map/ppermute | solution.py:380
  8.8 13.2 %collective-permute-start = (f32[48,128]{1,0:T(8,128)}, f32[48,128]{1,0:T(8,128)S(1)}, u32[]{:S(2)}, u32[]{:S(2)}) collective-permute-start(f32[48,128]{1,0:T(8,128)} %shard_map.120.t0_ref), channel_id=1, source_target_pairs={{0,32},{32,64},{64,96},{96,0},{1,33},{33,65},{65,97},{97,1},{2,34}... | collective-permute-start | bytes 73736 | tf_op jit(solution)/shard_map/ppermute | solution.py:380
  22.0 0.6 copy-start.4
  22.0 0.6 copy-start.5
  22.0 0.6 copy-start.6
  62.9 11.4 %copy-start = (bf16[1024,768]{1,0:T(8,128)(2,1)S(1)}, bf16[1024,768]{1,0:T(8,128)(2,1)}, u32[]{:S(2)}) copy-start(bf16[1024,768]{1,0:T(8,128)(2,1)} %get-tuple-element.31) | copy-start | bytes 4718596
  64.4 4.8 %collective-permute-start.5 = (f32[16,512]{1,0:T(8,128)S(1)}, f32[16,512]{1,0:T(8,128)S(1)}, u32[]{:S(2)}, u32[]{:S(2)}) collective-permute-start(f32[16,512]{1,0:T(8,128)S(1)} %get-tuple-element.34), channel_id=1, source_target_pairs={{0,96},{32,0},{64,32},{96,64},{1,97},{33,1},{65,33},{97,65},{2,98}... | collective-permute-start | bytes 98312 | tf_op jit(solution)/shard_map/ppermute | solution.py:380
  64.4 4.8 %collective-permute-start.4 = (f32[16,512]{1,0:T(8,128)S(1)}, f32[16,512]{1,0:T(8,128)S(1)}, u32[]{:S(2)}, u32[]{:S(2)}) collective-permute-start(f32[16,512]{1,0:T(8,128)S(1)} %get-tuple-element.35), channel_id=1, source_target_pairs={{0,64},{32,96},{64,0},{96,32},{1,65},{33,97},{65,1},{97,33},{2,66}... | collective-permute-start | bytes 98312 | tf_op jit(solution)/shard_map/ppermute | solution.py:380
  64.7 4.7 %collective-permute-start.3 = (f32[16,512]{1,0:T(8,128)S(1)}, f32[16,512]{1,0:T(8,128)S(1)}, u32[]{:S(2)}, u32[]{:S(2)}) collective-permute-start(f32[16,512]{1,0:T(8,128)S(1)} %get-tuple-element.36), channel_id=1, source_target_pairs={{0,32},{32,64},{64,96},{96,0},{1,33},{33,65},{65,97},{97,1},{2,34}... | collective-permute-start | bytes 98312 | tf_op jit(solution)/shard_map/ppermute | solution.py:380
  69.3 0.6 copy-start.1
  69.3 0.6 copy-start.2
  69.4 0.6 copy-start.3
  74.4 5.8 %collective-permute-start.6 = (bf16[64,8,896]{2,1,0:T(8,128)(2,1)S(1)}, bf16[64,8,896]{2,1,0:T(8,128)(2,1)}, u32[]{:S(2)}, u32[]{:S(2)}) collective-permute-start(bf16[64,8,896]{2,1,0:T(8,128)(2,1)S(1)} %fusion.3), channel_id=1, source_target_pairs={{0,32},{32,0},{1,33},{33,1},{2,34},{34,2},{3,35},{35,3},{4,36},{36... | collective-permute-start | bytes 2752520 | tf_op jit(solution)/shard_map/ppermute | solution.py:380
  82.5 24.5 %all-to-all-start = ((bf16[64,8,896]{2,1,0:T(8,128)(2,1)}), bf16[64,8,896]{2,1,0:T(8,128)(2,1)S(1)}, u32[]{:S(2)}, u32[]{:S(2)}) async-start(bf16[64,8,896]{2,1,0:T(8,128)(2,1)} %fusion), calls=%async_computation | async-start | bytes 1835008 | tf_op jit(solution)/shard_map/all_to_all | solution.py:395
  129.1 5.3 %collective-permute-start.7 = (bf16[64,8,896]{2,1,0:T(8,128)(2,1)S(1)}, bf16[64,8,896]{2,1,0:T(8,128)(2,1)S(1)}, u32[]{:S(2)}, u32[]{:S(2)}) collective-permute-start(bf16[64,8,896]{2,1,0:T(8,128)(2,1)S(1)} %all_to_all.10), channel_id=1, source_target_pairs={{0,32},{32,0},{1,33},{33,1},{2,34},{34,2},{3,35},{35,3},{4,36},{36... | collective-permute-start | bytes 2752520 | tf_op jit(solution)/shard_map/ppermute | solution.py:380

commit v2 on v1

--- a/solution.py
+++ b/solution.py
@@ -73,8 +73,19 @@
     return pl.BlockSpec(memory_space=pltpu.SMEM)
 
 
+def spread(w_ref, rows, source):
+    acc = None
+    for t in range(9):
+        r = iota((rows, 4), 0)
+        pick = jnp.where(source(r) == 4 * t + iota((rows, 4), 1), 1.0, 0.0).astype(BF16)
+        part = dot(pick, w_ref[t], 1, 0)
+        acc = part if acc is None else acc + part
+    return acc.astype(BF16)
+
+
 def conv_body(f_ref, w_ref, o_ref):
-    y = dot(w_ref[...], f_ref[...], 1, 1)
+    w72 = spread(w_ref, 72, lambda r: jnp.where(r % 8 < 4, r // 8 * 4 + r % 8, -1))
+    y = dot(w72, f_ref[...], 1, 1)
     tiles = []
     for ky in range(3):
         for h in range(8):
@@ -265,7 +276,7 @@
 
 def backward_body(
     s_ref, gz_ref, w_ref, x_ref, uk_ref, ut_ref, vt_ref, inv_ref, b_ref, c_ref, ep_ref, pw_ref,
-    o_ref,
+    o0_ref, o1_ref, o2_ref, o3_ref,
     wsel, gsel, wt, gt, ysc, hk, hv, padded,
 ):
     s = s_ref[0]
@@ -334,11 +345,21 @@
     line = jnp.concatenate([z] + pieces + [z], axis=1)
     for a in range(4):
         padded[a] = line[:, 256 * a : 256 * a + 512]
-    for k in range(4):
-        o_ref[k] = padded[(s + k) % 4]
-
-
-def output_body(g0_ref, g1_ref, g2_ref, g3_ref, f_ref, w_ref, o_ref, gc_ref):
+    for k, ref in enumerate((o0_ref, o1_ref, o2_ref, o3_ref)):
+        ref[...] = padded[(s + k) % 4]
+
+
+def output_body(g0_ref, g1_ref, g2_ref, g3_ref, f_ref, w_ref, loss_ref, o_ref, gc_ref):
+    def even_tap(r):
+        kx, q, o = r // 16, r % 16 // 4, r % 4
+        ky = jnp.where(q == 0, 1, jnp.where(q == 1, 0, 2))
+        return jnp.where(q == 2, -1, (ky * 3 + kx) * 4 + o)
+
+    def odd_tap(r):
+        kx, q, o = r // 16, r % 16 // 4, r % 4
+        return jnp.where(q == 3, -1, ((2 - q) * 3 + kx) * 4 + o)
+
+    w_back = (spread(w_ref, 48, even_tap), spread(w_ref, 48, odd_tap))
     g = (g0_ref[...] + g1_ref[...] + g2_ref[...] + g3_ref[...]).astype(BF16).astype(F32)
     left = iota((8, 128), 1) < 64
     tiles = []
@@ -364,16 +385,52 @@
         for kx in range(3):
             rows += [tile(i, kx), tile(other, kx)]
         gt = jnp.concatenate(rows, axis=0).astype(BF16)
-        o_ref[128 * a : 128 * a + 128, :] = dot(gt, w_ref[a % 2], 0, 0).astype(BF16)
+        o_ref[128 * a : 128 * a + 128, :] = dot(gt, w_back[a % 2], 0, 0).astype(BF16)
         part = dot(gt, f_ref[128 * a : 128 * a + 128, :], 1, 0)
         acc[a % 2] = part if acc[a % 2] is None else acc[a % 2] + part
     ev, od = acc
+    taps = [None] * 9
     for kx in range(3):
         et, epv = ev[16 * kx : 16 * kx + 8], ev[16 * kx + 8 : 16 * kx + 16]
         ot, on = od[16 * kx : 16 * kx + 8], od[16 * kx + 8 : 16 * kx + 16]
-        gc_ref[kx] = pltpu.roll(et, 4, 0) + on
-        gc_ref[3 + kx] = et + pltpu.roll(ot, 4, 0)
-        gc_ref[6 + kx] = pltpu.roll(epv, 4, 0) + ot
+        taps[kx] = pltpu.roll(et, 4, 0) + on
+        taps[3 + kx] = et + pltpu.roll(ot, 4, 0)
+        taps[6 + kx] = pltpu.roll(epv, 4, 0) + ot
+    upper = iota((8, 512), 0) < 4
+    rows = [
+        jnp.where(upper, taps[2 * j], pltpu.roll(taps[2 * j + 1], 4, 0)) for j in range(4)
+    ]
+    rows.append(jnp.where(upper, taps[8], 0.0))
+    put_sum(gc_ref, jnp.concatenate(rows, axis=0), loss_ref[0:1, 0:1])
+
+
+def put_sum(ref, conv, total):
+    hi, mid, lo = split3(total)
+    row = iota((40, 512), 0)
+    lane = iota((40, 512), 1)
+    loss = jnp.where(lane == 0, hi.astype(F32), 0.0)
+    loss = jnp.where(lane == 1, mid.astype(F32), loss)
+    loss = jnp.where(lane == 2, lo.astype(F32), loss)
+    ref[...] = jnp.where(row == 36, loss, jnp.where(row < 36, conv, 0.0)).astype(BF16)
+
+
+def sum_refs(refs):
+    acc = refs[0][...].astype(F32)
+    for ref in refs[1:]:
+        acc = acc + ref[...].astype(F32)
+    return acc, jnp.sum(acc[36:37, 0:128], axis=1, keepdims=True)
+
+
+def merge_body(*refs):
+    conv, total = sum_refs(refs[:-1])
+    put_sum(refs[-1], conv, total)
+
+
+def finish_body(*refs):
+    conv, total = sum_refs(refs[:-2])
+    for t in range(9):
+        refs[-2][t] = conv[4 * t : 4 * t + 4]
+    refs[-1][...] = jnp.broadcast_to(total * (1.0 / 32768.0), (8, 128))
 
 
 def shifted(x, axis, n, k):
@@ -381,44 +438,28 @@
 
 
 SLAB = ("xh", "core")
-CHIPS = ("xh", "z", "y", "xl")
-
-
-def reduced(parts):
-    n = parts.shape[-1]
-    core = lax.axis_index("core")
-    halves = parts.reshape(2, 64, 8, n)
-    mine = lax.dynamic_index_in_dim(halves, core, 0, keepdims=False)
-    other = lax.dynamic_index_in_dim(halves, 1 - core, 0, keepdims=False)
-    got = shifted(other, "core", 2, 1)
-    chip = (mine.astype(F32) + got.astype(F32)).astype(BF16)
-    pieces = lax.all_to_all(chip, CHIPS, split_axis=0, concat_axis=0, tiled=True)
-    return jnp.sum(pieces.astype(F32), 0)
-
-
-def gathered(block):
-    n = block.shape[-1]
-    same = jnp.broadcast_to(block[None], (64, 8, n))
-    half = lax.all_to_all(same, CHIPS, split_axis=0, concat_axis=0, tiled=True)
-    other = shifted(half, "core", 2, 1)
-    core = lax.axis_index("core")
-    return jnp.where(core == 0, half, other), jnp.where(core == 0, other, half)
+ALL = ("xh", "core", "z", "y", "xl")
+
+
+def summed(conv, axis, n, last):
+    parts = [conv] + [shifted(conv, axis, n, k) for k in range(1, n)]
+    if not last:
+        return call(merge_body, jax.ShapeDtypeStruct((40, 512), BF16), [vmem()] * n, vmem())(*parts)
+    return call(
+        finish_body,
+        (jax.ShapeDtypeStruct((9, 4, 512), F32), jax.ShapeDtypeStruct((8, 128), F32)),
+        [vmem()] * n,
+        (vmem(), vmem()),
+    )(*parts)
 
 
 def local(feats, labels, conv_w, embed_w, mod_table, qkv_w, out_w, proj_w, dino):
     slab = (lax.axis_index("xh") * 2 + lax.axis_index("core")).astype(jnp.int32).reshape(1)
     image = feats.reshape(1024, 512)
     taps = conv_w.transpose(0, 2, 1)
-    w72 = jnp.pad(taps, ((0, 0), (0, 4), (0, 0))).reshape(72, 512)
-    t3 = taps.reshape(3, 3, 4, 512)
-    none = jnp.zeros_like(t3[0])
-    w_even = jnp.stack([t3[1], t3[0], none, t3[2]], axis=1).reshape(48, 512)
-    w_odd = jnp.stack([t3[2], t3[1], t3[0], none], axis=1).reshape(48, 512)
-    w_back = jnp.stack([w_even, w_odd])
-
     part = call(
         conv_body, jax.ShapeDtypeStruct((48, 128), F32), [vmem(), vmem()], vmem()
-    )(image, w72)
+    )(image, taps)
     parts = [part] + [shifted(part, SLAB, 4, k) for k in (1, 2, 3)]
 
     mat, bexp, cexp, ep = pl.pallas_call(
@@ -472,11 +513,17 @@
         ],
     )(slab, *parts, mat, bexp, cexp, ep, proj_w, dino.reshape(256, 768))
 
+    parts = lax.all_to_all(gp.reshape(128, 8, 768), ALL, split_axis=0, concat_axis=0, tiled=True)
+    block = jnp.sum(parts.astype(F32), 0).astype(BF16)
+    same = jnp.broadcast_to(block[None], (128, 8, 768))
+    whole = lax.all_to_all(same, ALL, split_axis=0, concat_axis=0, tiled=True)
+    grad_proj = whole.reshape(1024, 768).astype(F32)
+
     pieces = call(
         backward_body,
-        jax.ShapeDtypeStruct((4, 16, 512), F32),
+        tuple([jax.ShapeDtypeStruct((16, 512), F32)] * 4),
         [smem()] + [vmem()] * 11,
-        vmem(),
+        tuple([vmem()] * 4),
         scratch=[
             pltpu.VMEM((8, 256, 128), BF16),
             pltpu.VMEM((8, 256, 128), BF16),
@@ -490,39 +537,20 @@
     )(slab, gz, w_all, x_all, uk, ut, vt, inv, bexp, cexp, ep, proj_w)
     grads = [pieces[0]] + [shifted(pieces[k], SLAB, 4, k) for k in (1, 2, 3)]
 
-    grad_image, gconv = call(
+    grad_image, conv = call(
         output_body,
-        (jax.ShapeDtypeStruct((1024, 512), BF16), jax.ShapeDtypeStruct((9, 8, 512), F32)),
-        [vmem()] * 6,
+        (jax.ShapeDtypeStruct((1024, 512), BF16), jax.ShapeDtypeStruct((40, 512), BF16)),
+        [vmem()] * 7,
         (vmem(), vmem()),
-    )(*grads, image, w_back)
-
-    conv_part = gconv.astype(BF16).reshape(9, 8, 4, 128).transpose(0, 2, 1, 3).reshape(36, 8, 128)
-    total = loss[0, 0]
-    lh, lm, ll = split3(total)
-    lane = jnp.arange(128)
-    loss_row = jnp.where(lane == 0, lh, jnp.where(lane == 1, lm, jnp.where(lane == 2, ll, 0)))
-    loss_part = jnp.broadcast_to(loss_row.astype(BF16), (1, 8, 128))
-    extra = jnp.concatenate([conv_part, loss_part, jnp.zeros((91, 8, 128), BF16)])
-    both = jnp.concatenate([gp.reshape(128, 8, 768), extra], axis=2)
-    block = reduced(both)
-    lsum = jnp.sum(block[0, 768:771])
-    lh, lm, ll = split3(lsum)
-    pos = (lax.axis_index(CHIPS) + 64 * lax.axis_index("core")) == 36
-    wide = jnp.arange(896)[None, :]
-    coded = jnp.where(wide == 768, lh, jnp.where(wide == 769, lm, ll)).astype(BF16)
-    is_loss = pos & (wide >= 768) & (wide < 771)
-    block = jnp.where(is_loss, coded, block.astype(BF16))
-    first, second = gathered(block)
-    grad_proj = jnp.concatenate([first[:, :, :768], second[:, :, :768]]).reshape(1024, 768).astype(F32)
-    conv = first[:36, :4, 768:].astype(F32).reshape(9, 4, 4, 128).transpose(0, 2, 1, 3)
-    grad_conv = conv.reshape(9, 4, 512).transpose(0, 2, 1)
-    loss_sum = jnp.sum(first[36, 0, 768:771].astype(F32))
+    )(*grads, image, taps, loss)
+    conv = summed(conv, "z", 4, False)
+    conv = summed(conv, "y", 4, False)
+    conv, loss = summed(conv, ("xh", "core", "xl"), 8, True)
     return (
         grad_image.reshape(1, 8, 128, 512),
         grad_proj,
-        grad_conv,
-        loss_sum / 32768.0,
+        conv.transpose(0, 2, 1),
+        loss[0, 0],
     )
 
 

time: 140 us -> 150 us (1.071)
  blocking collectives: 19.9 us -> 33.1 us
  starting transfers between devices: 26.9 us -> 33.5 us
  other arithmetic: 8.33 us -> 2.17 us
  Pallas kernels: 51.4 us -> 56.5 us
  between operations: 5.88 us -> 1.44 us
  waiting for transfers between devices: 20.8 us -> 16.5 us
    all_to_all x1, waiting for transfers between devices: 15.2 us -> 0.01 us  [local(): whole = lax.all_to_all(same, ALL, split_axis=0, concat_axis=0, tiled=True)]
    all_to_all x1, blocking collectives: 19.9 us -> 33.1 us  [local(): lax.all_to_all(gp.reshape(128, 8, 768), ALL, split_axis=0, concat_axis=0,...]
    ppermute x8 -> x19, starting transfers between devices: 17.7 us -> 29.1 us  [shifted(): return lax.ppermute(x, axis, [(i, (i + k) % n) for i in range(n)])]
    ppermute x8 -> x19, waiting for transfers between devices: 5.53 us -> 16.5 us  [shifted(): return lax.ppermute(x, axis, [(i, (i + k) % n) for i in range(n)])]
    all_to_all x1, starting transfers between devices: 9.26 us -> 4.41 us  [local(): whole = lax.all_to_all(same, ALL, split_axis=0, concat_axis=0, tiled=True)]
    pallas_call x1 -> x4, Pallas kernels: 20.4 us -> 25.1 us  [the longest x1 20.3 us: local(): call(backward_body, tuple([jax.ShapeDtypeStruct((16, 512), F32)] * 4), [s...]
    convert_element_type x3 -> x1, other arithmetic: 5.11 us -> 1.9 us  [local(): grad_proj = whole.reshape(1024, 768).astype(F32)]
    unnamed x14 -> x38, local copies, waits for them, and re-layouts: 1.2 us -> 3.8 us
  transfers between devices with their start and end apart: 9 -> 20, of which waited for: 5 -> 12; matrix products, arithmetic and copies ran while one was open for 1% -> 1% of each run, Pallas kernels for 6% -> 24%
where the time goes in v2:
time: 150 us; the launch traced here: 149 us
  Pallas kernels  56.5 us (38%)
  starting transfers between devices  33.5 us (22%)
  blocking collectives  33.1 us (22%)
  waiting for transfers between devices  16.5 us (11%)
  local copies, waits for them, and re-layouts  6.27 us (4%)
  other arithmetic  2.17 us (1%)
    all_to_all x1, blocking collectives, local(): lax.all_to_all(gp.reshape(128, 8, 768), ALL, split_axis=0, concat_axis=0,...  33.1 us
    ppermute x19, starting transfers between devices, shifted(): return lax.ppermute(x, axis, [(i, (i + k) % n) for i in range(n)])  29.1 us
    pallas_call x1, Pallas kernels, local(): call(backward_body, tuple([jax.ShapeDtypeStruct((16, 512), F32)] * 4), [s...  20.3 us
    pallas_call x1, Pallas kernels, local(): call(forward_body, (jax.ShapeDtypeStruct((1024, 768), BF16), jax.ShapeDty...  17.4 us
    ppermute x19, waiting for transfers between devices, shifted(): return lax.ppermute(x, axis, [(i, (i + k) % n) for i in range(n)])  16.5 us
    pallas_call x1, Pallas kernels, local(): pl.pallas_call(weights_body, out_shape=(jax.ShapeDtypeStruct((16, 16), F3...  8.04 us
    all_to_all x1, starting transfers between devices, local(): whole = lax.all_to_all(same, ALL, split_axis=0, concat_axis=0, tiled=True)  4.41 us
    unnamed x38, local copies, waits for them, and re-layouts  3.8 us
  transfers between devices with their start and end apart: 20, of which 12 were waited for; matrix products, arithmetic and copies ran while one was open for 1% of the time, Pallas kernels for 24%

profile of v2, /device:TPU:1, one launch (start us, length us, event | category | flops | bytes accessed | tf_op | source)
XLA Modules:
  0.0 149.5 jit_solution(981443769435439520)
XLA Ops:
  0.6 2.8 %shard_map.120.t0_ref = f32[48,128]{1,0:T(8,128)} custom-call(bf16[1024,512]{1,0:T(8,128)(2,1)} %bitcast.11, bf16[9,4,512]{2,1,0:T(4,128)(2,1)} %bitcast.15), custom_call_target="tpu_custom_call" | custom-call | tf_op jit(solution)/shard_map/pallas_call | solution.py:460
  3.4 1.4 collective-permute-start.2
  4.8 2.9 %collective-permute-start.1 = (f32[48,128]{1,0:T(8,128)}, f32[48,128]{1,0:T(8,128)S(1)}, u32[]{:S(2)}, u32[]{:S(2)}) collective-permute-start(f32[48,128]{1,0:T(8,128)} %shard_map.120.t0_ref), channel_id=1, source_target_pairs={{0,64},{32,96},{64,0},{96,32},{1,65},{33,97},{65,1},{97,33},{2,66}... | collective-permute-start | bytes 73736 | tf_op jit(solution)/shard_map/ppermute | solution.py:437
  7.7 2.9 %collective-permute-start = (f32[48,128]{1,0:T(8,128)}, f32[48,128]{1,0:T(8,128)S(1)}, u32[]{:S(2)}, u32[]{:S(2)}) collective-permute-start(f32[48,128]{1,0:T(8,128)} %shard_map.120.t0_ref), channel_id=1, source_target_pairs={{0,32},{32,64},{64,96},{96,0},{1,33},{33,65},{65,97},{97,1},{2,34}... | collective-permute-start | bytes 73736 | tf_op jit(solution)/shard_map/ppermute | solution.py:437
  11.2 8.0 %shard_map.121 = (f32[16,16]{1,0:T(8,128)}, f32[32,1024]{1,0:T(8,128)}, bf16[1024,1024]{1,0:T(8,128)(2,1)}, bf16[16,1024]{1,0:T(8,128)(2,1)}) custom-call(s32[1]{0:T(128)S(6)} %copy.13.lab_ref, bf16[16,1024]{1,0:T(8,128)(2,1)} %e_ref.1, bf16[1000,2048]{1,0:T(8,128)(2,1)} %mod_ref.1, bf16[1024,3072]{1,0:T(8,128)(2,1)} %qkv_ref.1, bf16[1024,1024]{1,0:T(8,128)(2,1)} %outw_ref.1), custom_call_target="tpu_custom_call" | custom-call | tf_op jit(solution)/shard_map/pallas_call | solution.py:465
  19.3 0.6 copy-done.16
  19.8 17.4 %shard_map.122 = (bf16[1024,768]{1,0:T(8,128)(2,1)}, bf16[256,768]{1,0:T(8,128)(2,1)}, f32[8,256,128]{2,1,0:T(8,128)}, bf16[8,256,128]{2,1,0:T(8,128)(2,1)}, bf1...) custom-call(s32[1]{0:T(128)} %bitcast.s_ref, ...), custom_call_target="tpu_custom_call" | custom-call | tf_op jit(solution)/shard_map/pallas_call | solution.py:493
  37.3 33.1 %all_to_all.10 = bf16[128,8,768]{2,1,0:T(8,128)(2,1)S(1)} all-to-all(bf16[128,8,768]{2,1,0:T(8,128)(2,1)} %bitcast.13), channel_id=1, replica_groups=mesh['xh'=2,'core'=2,'z'=4,'y'=4,'xl'=2] {'xh','core','z','y','xl'}, dimensions={0} | all-to-all | bytes 3145728 | tf_op jit(solution)/shard_map/all_to_all | solution.py:516
  70.4 0.3 reduce_sum.12
  70.7 1.3 broadcast_in_dim.2
  71.9 4.4 %all-to-all-start.1 = ((bf16[128,8,768]{2,1,0:T(8,128)(2,1)}), bf16[128,8,768]{2,1,0:T(8,128)(2,1)S(1)}, u32[]{:S(2)}, u32[]{:S(2)}) async-start(bf16[128,8,768]{2,1,0:T(8,128)(2,1)} %broadcast_in_dim.2), calls=%async_computation.1 | async-start | bytes 3145728 | tf_op jit(solution)/shard_map/all_to_all | solution.py:519
  76.3 20.3 %shard_map.123 = (f32[16,512]{1,0:T(8,128)}, f32[16,512]{1,0:T(8,128)}, f32[16,512]{1,0:T(8,128)}, f32[16,512]{1,0:T(8,128)}) custom-call(s32[1]{0:T(128)} %bitcast.s_ref, bf16[256,768]{1,0:T(8,128)(2,1)} %get-tuple-element.29.gz_ref, f32[8,256,128]{2,1,0:T(8,128)} %get-tuple-element.30.w_ref, bf16[8,256,128]{2,1,0:T(8,128)(2,1)} %get-tuple-element.31.x_ref, ...), custom_call_target="tpu_custom_call" | custom-call | tf_op jit(solution)/shard_map/pallas_call | solution.py:522
  96.7 3.2 %collective-permute-start.3 = (f32[16,512]{1,0:T(8,128)}, f32[16,512]{1,0:T(8,128)S(1)}, u32[]{:S(2)}, u32[]{:S(2)}) collective-permute-start(f32[16,512]{1,0:T(8,128)} %get-tuple-element.37), channel_id=1, source_target_pairs={{0,32},{32,64},{64,96},{96,0},{1,33},{33,65},{65,97},{97,1},{2,34}... | collective-permute-start | bytes 98312 | tf_op jit(solution)/shard_map/ppermute | solution.py:437
  99.9 1.1 collective-permute-start.4
  100.9 0.3 collective-permute-done.3.g1_ref
  101.2 3.1 %collective-permute-done.4.g2_ref = f32[16,512]{1,0:T(8,128)S(1)} collective-permute-done((f32[16,512]{1,0:T(8,128)}, f32[16,512]{1,0:T(8,128)S(1)}, u32[]{:S(2)}, u32[]{:S(2)}) %collective-permute-start.4) | collective-permute-done | bytes 32800 | tf_op jit(solution)/shard_map/ppermute | solution.py:437
  104.3 1.6 %collective-permute-done.5.g3_ref = f32[16,512]{1,0:T(8,128)S(1)} collective-permute-done((f32[16,512]{1,0:T(8,128)}, f32[16,512]{1,0:T(8,128)S(1)}, u32[]{:S(2)}, u32[]{:S(2)}) %collective-permute-start.5) | collective-permute-done | bytes 32800 | tf_op jit(solution)/shard_map/ppermute | solution.py:437
  106.0 0.6 copy-done.15
  106.6 3.2 %shard_map.124 = (bf16[1024,512]{1,0:T(8,128)(2,1)}, bf16[40,512]{1,0:T(8,128)(2,1)}) custom-call(f32[16,512]{1,0:T(8,128)} %get-tuple-element.36.g0_ref, f32[16,512]{1,0:T(8,128)} %copy-done.13, f32[16,512]{1,0:T(8,128)} %copy-done.14, f32[16,512]{1,0:T(8,128)} %copy-done.15, bf16[1024,512]{1,0:T(8,128)(2,1)} %bitcast.12, bf16[9,4,512]{2,1,0:T(4,128)(2,1)} %bitcast.16, ...), custom_call_target="tpu_custom_call" | custom-call | tf_op jit(solution)/shard_map/pallas_call | solution.py:540
  109.8 2.4 %collective-permute-start.8 = (bf16[40,512]{1,0:T(8,128)(2,1)}, bf16[40,512]{1,0:T(8,128)(2,1)S(1)}, u32[]{:S(2)}, u32[]{:S(2)}) collective-permute-start(bf16[40,512]{1,0:T(8,128)(2,1)} %get-tuple-element.43.refs_0_), channel_id=1, source_target_pairs={{0,24},{8,0},{16,8},{24,16},{1,25},{9,1},{17,9},{25,17},{2,26},{10... | collective-permute-start | bytes 122888 | tf_op jit(solution)/shard_map/ppermute | solution.py:437
  112.3 0.8 collective-permute-start.6
  113.1 0.5 collective-permute-done.8.refs_3_
  113.6 3.2 %collective-permute-done.7.refs_2_ = bf16[40,512]{1,0:T(8,128)(2,1)S(1)} collective-permute-done((bf16[40,512]{1,0:T(8,128)(2,1)}, bf16[40,512]{1,0:T(8,128)(2,1)S(1)}, u32[]{:S(2)}, u32[]{:S(2)}) %collective-permute-start.7) | collective-permute-done | bytes 40992 | tf_op jit(solution)/shard_map/ppermute | solution.py:437
  116.9 0.1 collective-permute-done.6.refs_1_
  117.0 0.5 copy-done.9
  117.5 0.6 copy-done.11
  118.1 1.5 %shard_map.125.refs_0_ = bf16[40,512]{1,0:T(8,128)(2,1)} custom-call(bf16[40,512]{1,0:T(8,128)(2,1)} %get-tuple-element.43.refs_0_, bf16[40,512]{1,0:T(8,128)(2,1)} %copy-done.11, bf16[40,512]{1,0:T(8,128)(2,1)} %copy-done.9, bf16[40,512]{1,0:T(8,128)(2,1)} %copy-done.7), custom_call_target="tpu_custom_call" | custom-call | tf_op jit(solution)/shard_map/pallas_call | solution.py:447
  119.7 2.6 %collective-permute-start.11 = (bf16[40,512]{1,0:T(8,128)(2,1)}, bf16[40,512]{1,0:T(8,128)(2,1)S(1)}, u32[]{:S(2)}, u32[]{:S(2)}) collective-permute-start(bf16[40,512]{1,0:T(8,128)(2,1)} %shard_map.125.refs_0_), channel_id=1, source_target_pairs={{0,6},{2,0},{4,2},{6,4},{1,7},{3,1},{5,3},{7,5},{8,14},{10,8},{12,... | collective-permute-start | bytes 122888 | tf_op jit(solution)/shard_map/ppermute | solution.py:437
  122.3 0.4 collective-permute-start.10
  122.7 0.6 collective-permute-start.9
  123.4 0.3 collective-permute-done.11.refs_3_
  123.7 3.2 %collective-permute-done.10.refs_2_ = bf16[40,512]{1,0:T(8,128)(2,1)S(1)} collective-permute-done((bf16[40,512]{1,0:T(8,128)(2,1)}, bf16[40,512]{1,0:T(8,128)(2,1)S(1)}, u32[]{:S(2)}, u32[]{:S(2)}) %collective-permute-start.10) | collective-permute-done | bytes 40992 | tf_op jit(solution)/shard_map/ppermute | solution.py:437
  126.9 0.4 collective-permute-done.9.refs_1_
  127.3 0.2 copy-done.10
  127.5 0.6 copy-done.12
  128.1 1.6 %shard_map.126.refs_0_ = bf16[40,512]{1,0:T(8,128)(2,1)} custom-call(bf16[40,512]{1,0:T(8,128)(2,1)} %shard_map.125.refs_0_, bf16[40,512]{1,0:T(8,128)(2,1)} %copy-done.12, bf16[40,512]{1,0:T(8,128)(2,1)} %copy-done.10, bf16[40,512]{1,0:T(8,128)(2,1)} %copy-done.8), custom_call_target="tpu_custom_call" | custom-call | tf_op jit(solution)/shard_map/pallas_call | solution.py:447
  129.7 3.5 %collective-permute-start.18 = (bf16[40,512]{1,0:T(8,128)(2,1)}, bf16[40,512]{1,0:T(8,128)(2,1)S(1)}, u32[]{:S(2)}, u32[]{:S(2)}) collective-permute-start(bf16[40,512]{1,0:T(8,128)(2,1)} %shard_map.126.refs_0_), channel_id=1, source_target_pairs={{0,97},{1,0},{32,1},{33,32},{64,33},{65,64},{96,65},{97,96},{2,99}... | collective-permute-start | bytes 122888 | tf_op jit(solution)/shard_map/ppermute | solution.py:437
  133.2 1.0 collective-permute-start.16
  134.2 1.8 %collective-permute-start.15 = (bf16[40,512]{1,0:T(8,128)(2,1)}, bf16[40,512]{1,0:T(8,128)(2,1)S(1)}, u32[]{:S(2)}, u32[]{:S(2)}) collective-permute-start(bf16[40,512]{1,0:T(8,128)(2,1)} %shard_map.126.refs_0_), channel_id=1, source_target_pairs={{0,64},{1,65},{32,96},{33,97},{64,0},{65,1},{96,32},{97,33},{2,66}... | collective-permute-start | bytes 122888 | tf_op jit(solution)/shard_map/ppermute | solution.py:437
  136.1 1.5 collective-permute-start.14
  137.5 3.0 %collective-permute-start.13 = (bf16[40,512]{1,0:T(8,128)(2,1)}, bf16[40,512]{1,0:T(8,128)(2,1)S(1)}, u32[]{:S(2)}, u32[]{:S(2)}) collective-permute-start(bf16[40,512]{1,0:T(8,128)(2,1)} %shard_map.126.refs_0_), channel_id=1, source_target_pairs={{0,32},{1,33},{32,64},{33,65},{64,96},{65,97},{96,0},{97,1},{2,34}... | collective-permute-start | bytes 122888 | tf_op jit(solution)/shard_map/ppermute | solution.py:437
  140.5 0.2 collective-permute-done.14.refs_3_
  140.7 1.2 collective-permute-done.13.refs_2_
  141.9 2.2 %collective-permute-done.12.refs_1_ = bf16[40,512]{1,0:T(8,128)(2,1)S(1)} collective-permute-done((bf16[40,512]{1,0:T(8,128)(2,1)}, bf16[40,512]{1,0:T(8,128)(2,1)S(1)}, u32[]{:S(2)}, u32[]{:S(2)}) %collective-permute-start.12) | collective-permute-done | bytes 40992 | tf_op jit(solution)/shard_map/ppermute | solution.py:437
  144.2 0.6 copy-done.6
  144.8 1.6 %shard_map.127 = (f32[9,4,512]{2,1,0:T(4,128)}, f32[8,128]{1,0:T(8,128)}) custom-call(bf16[40,512]{1,0:T(8,128)(2,1)} %shard_map.126.refs_0_, bf16[40,512]{1,0:T(8,128)(2,1)} %copy-done.6, bf16[40,512]{1,0:T(8,128)(2,1)} %copy-done.5, bf16[40,512]{1,0:T(8,128)(2,1)} %copy-done.4, bf16[40,512]{1,0:T(8,128)(2,1)} %copy-done.3, bf16[40,512]{1,0:T(8,128)(2,1)} %copy-done.2, ...), custom_call_target="tpu_custom_call" | custom-call | tf_op jit(solution)/shard_map/pallas_call | solution.py:448
  146.4 1.2 slice.3
  147.6 1.9 %bitcast_convert_fusion = f32[1024,768]{1,0:T(8,128)} fusion(bf16[128,8,768]{2,1,0:T(8,128)(2,1)S(1)} %all-to-all-done.1), kind=kLoop, calls=%fused_computation | loop fusion | flops 786432 | bytes 4718592 | tf_op jit(solution)/shard_map/convert_element_type | solution.py:520
  (43 shorter events, 0.2 us)
Async XLA Ops:
  3.4 15.8 %collective-permute-start.2 = (f32[48,128]{1,0:T(8,128)}, f32[48,128]{1,0:T(8,128)S(1)}, u32[]{:S(2)}, u32[]{:S(2)}) collective-permute-start(f32[48,128]{1,0:T(8,128)} %shard_map.120.t0_ref), channel_id=1, source_target_pairs={{0,96},{32,0},{64,32},{96,64},{1,97},{33,1},{65,33},{97,65},{2,98}... | collective-permute-start | bytes 73736 | tf_op jit(solution)/shard_map/ppermute | solution.py:437
  4.8 14.4 %collective-permute-start.1 = (f32[48,128]{1,0:T(8,128)}, f32[48,128]{1,0:T(8,128)S(1)}, u32[]{:S(2)}, u32[]{:S(2)}) collective-permute-start(f32[48,128]{1,0:T(8,128)} %shard_map.120.t0_ref), channel_id=1, source_target_pairs={{0,64},{32,96},{64,0},{96,32},{1,65},{33,97},{65,1},{97,33},{2,66}... | collective-permute-start | bytes 73736 | tf_op jit(solution)/shard_map/ppermute | solution.py:437
  7.7 11.6 %collective-permute-start = (f32[48,128]{1,0:T(8,128)}, f32[48,128]{1,0:T(8,128)S(1)}, u32[]{:S(2)}, u32[]{:S(2)}) collective-permute-start(f32[48,128]{1,0:T(8,128)} %shard_map.120.t0_ref), channel_id=1, source_target_pairs={{0,32},{32,64},{64,96},{96,0},{1,33},{33,65},{65,97},{97,1},{2,34}... | collective-permute-start | bytes 73736 | tf_op jit(solution)/shard_map/ppermute | solution.py:437
  19.2 0.6 copy-start.16
  19.2 0.6 copy-start.17
  19.2 0.6 copy-start.18
  71.9 75.7 %all-to-all-start.1 = ((bf16[128,8,768]{2,1,0:T(8,128)(2,1)}), bf16[128,8,768]{2,1,0:T(8,128)(2,1)S(1)}, u32[]{:S(2)}, u32[]{:S(2)}) async-start(bf16[128,8,768]{2,1,0:T(8,128)(2,1)} %broadcast_in_dim.2), calls=%async_computation.1 | async-start | bytes 3145728 | tf_op jit(solution)/shard_map/all_to_all | solution.py:519
  96.7 4.5 %collective-permute-start.3 = (f32[16,512]{1,0:T(8,128)}, f32[16,512]{1,0:T(8,128)S(1)}, u32[]{:S(2)}, u32[]{:S(2)}) collective-permute-start(f32[16,512]{1,0:T(8,128)} %get-tuple-element.37), channel_id=1, source_target_pairs={{0,32},{32,64},{64,96},{96,0},{1,33},{33,65},{65,97},{97,1},{2,34}... | collective-permute-start | bytes 98312 | tf_op jit(solution)/shard_map/ppermute | solution.py:437
  99.9 4.5 %collective-permute-start.4 = (f32[16,512]{1,0:T(8,128)}, f32[16,512]{1,0:T(8,128)S(1)}, u32[]{:S(2)}, u32[]{:S(2)}) collective-permute-start(f32[16,512]{1,0:T(8,128)} %get-tuple-element.38), channel_id=1, source_target_pairs={{0,64},{32,96},{64,0},{96,32},{1,65},{33,97},{65,1},{97,33},{2,66}... | collective-permute-start | bytes 98312 | tf_op jit(solution)/shard_map/ppermute | solution.py:437
  100.9 5.1 %collective-permute-start.5 = (f32[16,512]{1,0:T(8,128)}, f32[16,512]{1,0:T(8,128)S(1)}, u32[]{:S(2)}, u32[]{:S(2)}) collective-permute-start(f32[16,512]{1,0:T(8,128)} %get-tuple-element.39), channel_id=1, source_target_pairs={{0,96},{32,0},{64,32},{96,64},{1,97},{33,1},{65,33},{97,65},{2,98}... | collective-permute-start | bytes 98312 | tf_op jit(solution)/shard_map/ppermute | solution.py:437
  101.2 4.8 %copy-start.13 = (f32[16,512]{1,0:T(8,128)}, f32[16,512]{1,0:T(8,128)S(1)}, u32[]{:S(2)}) copy-start(f32[16,512]{1,0:T(8,128)S(1)} %collective-permute-done.3.g1_ref) | copy-start | bytes 98308
  104.3 1.7 %copy-start.14 = (f32[16,512]{1,0:T(8,128)}, f32[16,512]{1,0:T(8,128)S(1)}, u32[]{:S(2)}) copy-start(f32[16,512]{1,0:T(8,128)S(1)} %collective-permute-done.4.g2_ref) | copy-start | bytes 98308
  106.0 0.6 copy-start.15
  109.8 3.8 %collective-permute-start.8 = (bf16[40,512]{1,0:T(8,128)(2,1)}, bf16[40,512]{1,0:T(8,128)(2,1)S(1)}, u32[]{:S(2)}, u32[]{:S(2)}) collective-permute-start(bf16[40,512]{1,0:T(8,128)(2,1)} %get-tuple-element.43.refs_0_), channel_id=1, source_target_pairs={{0,24},{8,0},{16,8},{24,16},{1,25},{9,1},{17,9},{25,17},{2,26},{10... | collective-permute-start | bytes 122888 | tf_op jit(solution)/shard_map/ppermute | solution.py:437
  112.2 4.7 %collective-permute-start.7 = (bf16[40,512]{1,0:T(8,128)(2,1)}, bf16[40,512]{1,0:T(8,128)(2,1)S(1)}, u32[]{:S(2)}, u32[]{:S(2)}) collective-permute-start(bf16[40,512]{1,0:T(8,128)(2,1)} %get-tuple-element.43.refs_0_), channel_id=1, source_target_pairs={{0,16},{8,24},{16,0},{24,8},{1,17},{9,25},{17,1},{25,9},{2,18},{10... | collective-permute-start | bytes 122888 | tf_op jit(solution)/shard_map/ppermute | solution.py:437
  112.3 4.7 %collective-permute-start.6 = (bf16[40,512]{1,0:T(8,128)(2,1)}, bf16[40,512]{1,0:T(8,128)(2,1)S(1)}, u32[]{:S(2)}, u32[]{:S(2)}) collective-permute-start(bf16[40,512]{1,0:T(8,128)(2,1)} %get-tuple-element.43.refs_0_), channel_id=1, source_target_pairs={{0,8},{8,16},{16,24},{24,0},{1,9},{9,17},{17,25},{25,1},{2,10},{10... | collective-permute-start | bytes 122888 | tf_op jit(solution)/shard_map/ppermute | solution.py:437
  113.6 3.4 %copy-start.7 = (bf16[40,512]{1,0:T(8,128)(2,1)}, bf16[40,512]{1,0:T(8,128)(2,1)S(1)}, u32[]{:S(2)}) copy-start(bf16[40,512]{1,0:T(8,128)(2,1)S(1)} %collective-permute-done.8.refs_3_) | copy-start | bytes 122884
  116.9 0.6 copy-start.9
  117.5 0.6 copy-start.11
  119.7 4.0 %collective-permute-start.11 = (bf16[40,512]{1,0:T(8,128)(2,1)}, bf16[40,512]{1,0:T(8,128)(2,1)S(1)}, u32[]{:S(2)}, u32[]{:S(2)}) collective-permute-start(bf16[40,512]{1,0:T(8,128)(2,1)} %shard_map.125.refs_0_), channel_id=1, source_target_pairs={{0,6},{2,0},{4,2},{6,4},{1,7},{3,1},{5,3},{7,5},{8,14},{10,8},{12,... | collective-permute-start | bytes 122888 | tf_op jit(solution)/shard_map/ppermute | solution.py:437
  122.3 4.6 %collective-permute-start.10 = (bf16[40,512]{1,0:T(8,128)(2,1)}, bf16[40,512]{1,0:T(8,128)(2,1)S(1)}, u32[]{:S(2)}, u32[]{:S(2)}) collective-permute-start(bf16[40,512]{1,0:T(8,128)(2,1)} %shard_map.125.refs_0_), channel_id=1, source_target_pairs={{0,4},{2,6},{4,0},{6,2},{1,5},{3,7},{5,1},{7,3},{8,12},{10,14},{12... | collective-permute-start | bytes 122888 | tf_op jit(solution)/shard_map/ppermute | solution.py:437
  122.7 4.6 %collective-permute-start.9 = (bf16[40,512]{1,0:T(8,128)(2,1)}, bf16[40,512]{1,0:T(8,128)(2,1)S(1)}, u32[]{:S(2)}, u32[]{:S(2)}) collective-permute-start(bf16[40,512]{1,0:T(8,128)(2,1)} %shard_map.125.refs_0_), channel_id=1, source_target_pairs={{0,2},{2,4},{4,6},{6,0},{1,3},{3,5},{5,7},{7,1},{8,10},{10,12},{12... | collective-permute-start | bytes 122888 | tf_op jit(solution)/shard_map/ppermute | solution.py:437
  123.7 3.6 %copy-start.8 = (bf16[40,512]{1,0:T(8,128)(2,1)}, bf16[40,512]{1,0:T(8,128)(2,1)S(1)}, u32[]{:S(2)}) copy-start(bf16[40,512]{1,0:T(8,128)(2,1)S(1)} %collective-permute-done.11.refs_3_) | copy-start | bytes 122884
  126.9 0.6 copy-start.10
  127.5 0.6 copy-start.12
  129.7 7.9 %collective-permute-start.18 = (bf16[40,512]{1,0:T(8,128)(2,1)}, bf16[40,512]{1,0:T(8,128)(2,1)S(1)}, u32[]{:S(2)}, u32[]{:S(2)}) collective-permute-start(bf16[40,512]{1,0:T(8,128)(2,1)} %shard_map.126.refs_0_), channel_id=1, source_target_pairs={{0,97},{1,0},{32,1},{33,32},{64,33},{65,64},{96,65},{97,96},{2,99}... | collective-permute-start | bytes 122888 | tf_op jit(solution)/shard_map/ppermute | solution.py:437
  133.2 7.3 %collective-permute-start.17 = (bf16[40,512]{1,0:T(8,128)(2,1)}, bf16[40,512]{1,0:T(8,128)(2,1)S(1)}, u32[]{:S(2)}, u32[]{:S(2)}) collective-permute-start(bf16[40,512]{1,0:T(8,128)(2,1)} %shard_map.126.refs_0_), channel_id=1, source_target_pairs={{0,96},{1,97},{32,0},{33,1},{64,32},{65,33},{96,64},{97,65},{2,98}... | collective-permute-start | bytes 122888 | tf_op jit(solution)/shard_map/ppermute | solution.py:437
  133.2 7.3 %collective-permute-start.16 = (bf16[40,512]{1,0:T(8,128)(2,1)}, bf16[40,512]{1,0:T(8,128)(2,1)S(1)}, u32[]{:S(2)}, u32[]{:S(2)}) collective-permute-start(bf16[40,512]{1,0:T(8,128)(2,1)} %shard_map.126.refs_0_), channel_id=1, source_target_pairs={{0,65},{1,96},{32,97},{33,0},{64,1},{65,32},{96,33},{97,64},{2,67}... | collective-permute-start | bytes 122888 | tf_op jit(solution)/shard_map/ppermute | solution.py:437
  134.2 6.3 %collective-permute-start.15 = (bf16[40,512]{1,0:T(8,128)(2,1)}, bf16[40,512]{1,0:T(8,128)(2,1)S(1)}, u32[]{:S(2)}, u32[]{:S(2)}) collective-permute-start(bf16[40,512]{1,0:T(8,128)(2,1)} %shard_map.126.refs_0_), channel_id=1, source_target_pairs={{0,64},{1,65},{32,96},{33,97},{64,0},{65,1},{96,32},{97,33},{2,66}... | collective-permute-start | bytes 122888 | tf_op jit(solution)/shard_map/ppermute | solution.py:437
  136.1 4.7 %collective-permute-start.14 = (bf16[40,512]{1,0:T(8,128)(2,1)}, bf16[40,512]{1,0:T(8,128)(2,1)S(1)}, u32[]{:S(2)}, u32[]{:S(2)}) collective-permute-start(bf16[40,512]{1,0:T(8,128)(2,1)} %shard_map.126.refs_0_), channel_id=1, source_target_pairs={{0,33},{1,64},{32,65},{33,96},{64,97},{65,0},{96,1},{97,32},{2,35}... | collective-permute-start | bytes 122888 | tf_op jit(solution)/shard_map/ppermute | solution.py:437
  137.5 6.6 %copy-start = (bf16[40,512]{1,0:T(8,128)(2,1)}, bf16[40,512]{1,0:T(8,128)(2,1)S(1)}, u32[]{:S(2)}) copy-start(bf16[40,512]{1,0:T(8,128)(2,1)S(1)} %collective-permute-done.18.refs_7_) | copy-start | bytes 122884
  137.5 4.4 %collective-permute-start.13 = (bf16[40,512]{1,0:T(8,128)(2,1)}, bf16[40,512]{1,0:T(8,128)(2,1)S(1)}, u32[]{:S(2)}, u32[]{:S(2)}) collective-permute-start(bf16[40,512]{1,0:T(8,128)(2,1)} %shard_map.126.refs_0_), channel_id=1, source_target_pairs={{0,32},{1,33},{32,64},{33,65},{64,96},{65,97},{96,0},{97,1},{2,34}... | collective-permute-start | bytes 122888 | tf_op jit(solution)/shard_map/ppermute | solution.py:437
  140.5 3.6 %copy-start.1 = (bf16[40,512]{1,0:T(8,128)(2,1)}, bf16[40,512]{1,0:T(8,128)(2,1)S(1)}, u32[]{:S(2)}) copy-start(bf16[40,512]{1,0:T(8,128)(2,1)S(1)} %collective-permute-done.17.refs_6_) | copy-start | bytes 122884
  140.5 3.6 %collective-permute-start.12 = (bf16[40,512]{1,0:T(8,128)(2,1)}, bf16[40,512]{1,0:T(8,128)(2,1)S(1)}, u32[]{:S(2)}, u32[]{:S(2)}) collective-permute-start(bf16[40,512]{1,0:T(8,128)(2,1)} %shard_map.126.refs_0_), channel_id=1, source_target_pairs={{0,1},{1,32},{32,33},{33,64},{64,65},{65,96},{96,97},{97,0},{2,3},... | collective-permute-start | bytes 122888 | tf_op jit(solution)/shard_map/ppermute | solution.py:437
  140.5 3.6 %copy-start.2 = (bf16[40,512]{1,0:T(8,128)(2,1)}, bf16[40,512]{1,0:T(8,128)(2,1)S(1)}, u32[]{:S(2)}) copy-start(bf16[40,512]{1,0:T(8,128)(2,1)S(1)} %collective-permute-done.16.refs_5_) | copy-start | bytes 122884
  140.5 3.6 %copy-start.3 = (bf16[40,512]{1,0:T(8,128)(2,1)}, bf16[40,512]{1,0:T(8,128)(2,1)S(1)}, u32[]{:S(2)}) copy-start(bf16[40,512]{1,0:T(8,128)(2,1)S(1)} %collective-permute-done.15.refs_4_) | copy-start | bytes 122884
  140.7 3.4 %copy-start.4 = (bf16[40,512]{1,0:T(8,128)(2,1)}, bf16[40,512]{1,0:T(8,128)(2,1)S(1)}, u32[]{:S(2)}) copy-start(bf16[40,512]{1,0:T(8,128)(2,1)S(1)} %collective-permute-done.14.refs_3_) | copy-start | bytes 122884
  141.9 2.3 %copy-start.5 = (bf16[40,512]{1,0:T(8,128)(2,1)}, bf16[40,512]{1,0:T(8,128)(2,1)S(1)}, u32[]{:S(2)}) copy-start(bf16[40,512]{1,0:T(8,128)(2,1)S(1)} %collective-permute-done.13.refs_2_) | copy-start | bytes 122884
  144.2 0.6 copy-start.6
